TPU v7x, 512 devices: a whole 4x4x16 slice. The times are simulated.
512 devices in a mesh: ctx: 64 (over x, z_lo, core), head: 8 (over y, z_hi).
Axes of the slice: x: 4, y: 4, z: 16 (z_hi: 2, z_lo: 8; z = z_hi * 8 + z_lo), core: 2. Of those that a mesh axis runs over, the one named last changes fastest.
Arguments:
- query_heads: bfloat16 [8192, 64, 576], P('ctx', 'head'), may hold values from -16 to 16
- key_latent: bfloat16 [8192, 576], P('ctx'), may hold values from -6 to 6
- doc_start: int32 [8192], P('ctx'), may hold values from 0 to 8191, as said below
- out_grad: bfloat16 [8192, 64, 512], P('ctx', 'head'), may hold values from -12 to 12
Outputs:
- attention: bfloat16 [8192, 64, 512], P('ctx', 'head')
- d_query: bfloat16 [8192, 64, 576], P('ctx', 'head')
- d_key: float32 [8192, 576], P(('ctx', 'head'))
Inputs may be any that keep to these rules, and one draw needn't show every extreme that they name: doc_start[t] <= t; doc_start[t] is t or doc_start[t - 1]; every document holds at most 256 tokens, and some document holds exactly 256.
All inputs are finite; a program needn't handle non-finite values.
Results may differ from a plain program's by a relative error of at most 0.013.
Values may be sent and summed in bfloat16 or wider, within the bound.
No kernel may reach another device: no remote copies, remote signals or barrier semaphores. Data moves between devices by JAX's collectives and lax.ppermute only.
A program may use at most 64 MiB of HBM per device.

v0:
```python
from functools import partial

import jax
import jax.numpy as jnp
from jax import lax
from jax.sharding import PartitionSpec as P

MAXDOC = 256


score_scale = 192 ** (-0.5)


def shifted(value, axis, steps):
    count = lax.axis_size(axis)
    leading, last = (max(0, -steps), min(count, count - steps))
    return lax.ppermute(value, axis, [(source, source + steps) for source in range(leading, last)])


def in_blocks(x, dim, devices):
    dims = x.shape
    pieces = x.reshape(*dims[:dim], devices, dims[dim] // devices, *dims[dim + 1 :])
    return jnp.moveaxis(pieces, dim, 0)


def sent_and_summed(x, axis, dim):
    devices = lax.axis_size(axis)
    pieces = lax.all_to_all(in_blocks(x, dim, devices), axis, 0, 0, tiled=True)
    return jnp.sum(pieces.astype(jnp.float32), axis=0)


def block_scores(query_heads, key_block, key_pos, query_pos, doc_start):
    scores = (
        jnp.einsum("thd,kd->thk", query_heads, key_block, preferred_element_type=jnp.float32)
        * score_scale
    )
    visible = (key_pos[None, :] >= doc_start[:, None]) & (key_pos[None, :] <= query_pos[:, None])
    return jnp.where(visible[:, None, :], scores, -jnp.inf)


def value_product(out_grad, key_block):
    latent_width = out_grad.shape[2]
    return jnp.einsum(
        "thc,kc->thk", out_grad, key_block[:, :latent_width], preferred_element_type=jnp.float32
    )


def block_grads(query_heads, out_grad, key_block, weights, dscore):
    latent_width = out_grad.shape[2]
    query_part = jnp.einsum("thk,kd->thd", dscore, key_block, preferred_element_type=jnp.float32)
    from_scores = jnp.einsum("thk,thd->kd", dscore, query_heads, preferred_element_type=jnp.float32)
    from_values = jnp.einsum("thk,thc->kc", weights, out_grad, preferred_element_type=jnp.float32)
    padding = key_block.shape[1] - latent_width
    return (query_part, from_scores + jnp.pad(from_values, ((0, 0), (0, padding))))


def send_back(partials, reach):
    summed = partials[reach]
    for offset in range(1, reach + 1):
        summed = summed + shifted(
            partials[reach - offset].astype(jnp.bfloat16), "ctx", -offset
        ).astype(jnp.float32)
    return summed


def shards(query_heads, key_latent, doc_start, out_grad):
    block_rows = key_latent.shape[0]
    head_count = query_heads.shape[1]
    latent_width = out_grad.shape[2]
    reach = (MAXDOC + block_rows - 2) // block_rows
    ctx_index = lax.axis_index("ctx")
    local_rows = jnp.arange(block_rows, dtype=jnp.int32)
    query_pos = ctx_index * block_rows + local_rows
    key_blocks = [shifted(key_latent, "ctx", offset) for offset in range(reach, 0, -1)]
    key_blocks.append(key_latent)
    earliest = jnp.min(doc_start)
    score_list = []
    live_list = []
    for number, key_block in enumerate(key_blocks):
        key_pos = (ctx_index - reach + number) * block_rows + local_rows
        is_live = earliest <= (ctx_index - reach + number + 1) * block_rows - 1
        compute = partial(block_scores, query_heads, key_block, key_pos, query_pos, doc_start)
        scores = compute()
        score_list.append(scores)
        live_list.append(is_live)
    top = score_list[0].max(axis=2, keepdims=True)
    for scores in score_list[1:]:
        top = jnp.maximum(top, scores.max(axis=2, keepdims=True))
    expon_list = [jnp.exp(scores - top) for scores in score_list]
    totals = expon_list[0].sum(axis=2, keepdims=True)
    for expon in expon_list[1:]:
        totals = totals + expon.sum(axis=2, keepdims=True)
    prob_list = [expon / totals for expon in expon_list]
    weight_list = [prob.astype(jnp.bfloat16) for prob in prob_list]
    output = jnp.zeros((block_rows, head_count, latent_width), jnp.float32)
    for weights, key_block in zip(weight_list, key_blocks):
        output = output + jnp.einsum(
            "thk,kc->thc", weights, key_block[:, :latent_width], preferred_element_type=jnp.float32
        )
    attention = output.astype(jnp.bfloat16)
    dprob_list = []
    for number, key_block in enumerate(key_blocks):
        compute = partial(value_product, out_grad, key_block)
        dprob = compute()
        dprob_list.append(dprob)
    row_delta = jnp.zeros((block_rows, head_count, 1), jnp.float32)
    for prob, dprob in zip(prob_list, dprob_list):
        row_delta = row_delta + jnp.sum(prob * dprob, axis=2, keepdims=True)
    query_grad = jnp.zeros(query_heads.shape, jnp.float32)
    partials = []
    for number, key_block in enumerate(key_blocks):
        dscore = (score_scale * prob_list[number] * (dprob_list[number] - row_delta)).astype(
            jnp.bfloat16
        )
        compute = partial(
            block_grads, query_heads, out_grad, key_block, weight_list[number], dscore
        )
        query_part, key_part = compute()
        query_grad = query_grad + query_part
        partials.append(key_part)
    d_query = query_grad.astype(jnp.bfloat16)
    owned = send_back(partials, reach)
    d_key = sent_and_summed(owned.astype(jnp.bfloat16), "head", 0)
    return (attention, d_query, d_key)


def solution(mesh):
    return jax.shard_map(
        shards,
        mesh=mesh,
        in_specs=(P("ctx", "head", None), P("ctx", None), P("ctx"), P("ctx", "head", None)),
        out_specs=(P("ctx", "head", None), P("ctx", "head", None), P(("ctx", "head"), None)),
        check_vma=False,
    )
```

profile of v0, /device:TPU:6, one launch (start us, length us, event | category | flops | bytes accessed | tf_op | source)
XLA Modules:
  0.0 71.6 jit_solution(6694049808467562605)
XLA Ops:
  0.7 2.1 %collective-permute-start.1 = (bf16[128,576]{0,1:T(8,128)(2,1)}, bf16[128,576]{0,1:T(8,128)(2,1)S(1)}, u32[]{:S(2)}, u32[]{:S(2)}) collective-permute-start(bf16[128,576]{0,1:T(8,128)(2,1)} %param.5), channel_id=1, source_target_pairs={{0,8},{8,16},{16,24},{24,32},{32,40},{40,48},{48,56},{56,64},{64,7... | collective-permute-start | bytes 442376 | tf_op jit(solution)/shard_map/ppermute | solution.py:17
  2.7 3.8 %collective-permute-start = (bf16[128,576]{0,1:T(8,128)(2,1)}, bf16[128,576]{0,1:T(8,128)(2,1)S(1)}, u32[]{:S(2)}, u32[]{:S(2)}) collective-permute-start(bf16[128,576]{0,1:T(8,128)(2,1)} %param.5), channel_id=1, source_target_pairs={{0,16},{8,24},{16,32},{24,40},{32,48},{40,56},{48,64},{56,72},{64,... | collective-permute-start | bytes 442376 | tf_op jit(solution)/shard_map/ppermute | solution.py:17
  6.6 0.8 %compare_and_fusion.2 = (pred[128,128]{0,1:T(8,128)(4,1)S(1)}, pred[128,128]{0,1:T(8,128)(4,1)S(1)}, pred[128,128]{0,1:T(8,128)(4,1)S(1)}) fusion(s32[128]{0:T(128)S(1)} %get-tuple-element.29, s32[128]{0:T(128)} %param.6, s32[128]{0:T(128)S(1)} %iota_add_fusion.2, s32[128]{0:T(128)S(1)} %get-tuple-element.28), kind=kLoop, calls=%fused_computation.69 | loop fusion | flops 147456 | bytes 51200 | tf_op jit(solution)/shard_map/and | solution.py:37
  7.4 1.3 %fusion.49 = (f32[128,8]{0,1:T(8,128)S(1)}, f32[128,8,128]{0,2,1:T(8,128)S(1)}) fusion(bf16[128,8,576]{0,2,1:T(8,128)(2,1)S(1)} %copy-done, bf16[128,576]{0,1:T(8,128)(2,1)} %param.5, pred[128,128]{0,1:T(8,128)(4,1)S(1)} %get-tuple-element.19), kind=kOutput, calls=%fused_computation.76 | convolution fusion | flops 151387136 | bytes 1871872 | tf_op jit(solution)/shard_map/thd,kd->thk/dot_general | solution.py:34
  8.8 0.8 %fusion.17 = f32[128,8,128]{0,2,1:T(8,128)S(1)} fusion(bf16[128,8,512]{2,1,0:T(8,128)(2,1)S(1)} %copy-done.1, bf16[128,576]{0,1:T(8,128)(2,1)S(1)} %copy-done.10), kind=kOutput, calls=%fused_computation.37 | convolution fusion | flops 134217728 | bytes 1703936 | tf_op jit(solution)/shard_map/thc,kc->thk/dot_general | solution.py:43
  9.5 10.7 %collective-permute-done = bf16[128,576]{0,1:T(8,128)(2,1)S(1)} collective-permute-done((bf16[128,576]{0,1:T(8,128)(2,1)}, bf16[128,576]{0,1:T(8,128)(2,1)S(1)}, u32[]{:S(2)}, u32[]{:S(2)}) %collective-permute-start) | collective-permute-done | bytes 147488 | tf_op jit(solution)/shard_map/ppermute | solution.py:17
  20.2 0.4 fusion.50
  20.7 0.4 fusion.51
  21.4 0.7 %convolution_bitcast_fusion.3 = f32[128,512]{0,1:T(8,128)S(1)} fusion(bf16[128,8,512]{2,1,0:T(8,128)(2,1)S(1)} %copy-done.1, f32[128,8,128]{0,2,1:T(8,128)S(1)} %get-tuple-element.24, f32[128,8]{0,1:T(8,128)S(1)} %add_add_fusion.1, f32[128,8]{0,1:T(8,128)S(1)} %maximum_maximum_fusion), kind=kOutput, calls=%fused_computation.11 | convolution fusion | flops 134610944 | bytes 1843200 | tf_op jit(solution)/shard_map/thk,thc->kc/dot_general | solution.py:52
  22.1 0.7 %convolution_bitcast_fusion.4 = f32[128,512]{0,1:T(8,128)S(1)} fusion(bf16[128,8,512]{2,1,0:T(8,128)(2,1)S(1)} %copy-done.1, f32[128,8,128]{0,2,1:T(8,128)S(1)} %get-tuple-element.26, f32[128,8]{0,1:T(8,128)S(1)} %add_add_fusion.1, f32[128,8]{0,1:T(8,128)S(1)} %maximum_maximum_fusion), kind=kOutput, calls=%fused_computation.12 | convolution fusion | flops 134610944 | bytes 1843200 | tf_op jit(solution)/shard_map/thk,thc->kc/dot_general | solution.py:52
  22.8 0.5 fusion.32
  23.3 0.8 %fusion.21 = f32[128,8,128]{0,2,1:T(8,128)S(1)} fusion(bf16[128,8,512]{2,1,0:T(8,128)(2,1)S(1)} %copy-done.1, bf16[128,576]{0,1:T(8,128)(2,1)S(1)} %collective-permute-done), kind=kOutput, calls=%fused_computation.41 | convolution fusion | flops 134217728 | bytes 1703936 | tf_op jit(solution)/shard_map/thc,kc->thk/dot_general | solution.py:43
  24.1 1.0 %multiply_reduce_fusion.1 = (f32[128,8]{0,1:T(8,128)S(1)}, f32[128,8]{0,1:T(8,128)S(1)}, f32[128,8]{0,1:T(8,128)S(1)}, f32[128,8,128]{0,2,1:T(8,128)S(1)}) fusion(f32[128,8]{0,1:T(8,128)S(1)} %add_add_fusion.1, f32[128,8,128]{0,2,1:T(8,128)S(1)} %get-tuple-element.26, f32[128,8]{0,1:T(8,128)S(1)} %maximum_maximum_fusion, f32[128,8,128]{0,2,1:T(8,128)S(1)} %fusion.21, ...), kind=kOutput, calls=%fused_computation.23 | convolution fusion | flops 135787520 | bytes 4345856 | tf_op jit(solution)/shard_map/thc,kc->thk/dot_general | solution.py:43
  25.1 0.4 multiply_convert_fusion.2
  25.6 0.5 fusion.6
  26.1 4.3 %collective-permute-start.3 = (bf16[128,576]{0,1:T(8,128)(2,1)S(1)}, bf16[128,576]{0,1:T(8,128)(2,1)S(1)}, u32[]{:S(2)}, u32[]{:S(2)}) collective-permute-start(bf16[128,576]{0,1:T(8,128)(2,1)S(1)} %fusion.6), channel_id=1, source_target_pairs={{16,0},{24,8},{32,16},{40,24},{48,32},{56,40},{64,48},{72,56},{80,... | collective-permute-start | bytes 442376 | tf_op jit(solution)/shard_map/ppermute | solution.py:17
  30.4 0.5 fusion.7
  30.9 1.9 %collective-permute-start.2 = (bf16[128,576]{0,1:T(8,128)(2,1)S(1)}, bf16[128,576]{0,1:T(8,128)(2,1)S(1)}, u32[]{:S(2)}, u32[]{:S(2)}) collective-permute-start(bf16[128,576]{0,1:T(8,128)(2,1)S(1)} %fusion.7), channel_id=1, source_target_pairs={{8,0},{16,8},{24,16},{32,24},{40,32},{48,40},{56,48},{64,56},{72,6... | collective-permute-start | bytes 442376 | tf_op jit(solution)/shard_map/ppermute | solution.py:17
  32.8 0.5 fusion.23
  33.3 0.4 copy-done.13
  33.7 0.5 fusion.37
  34.2 0.4 copy-done.8
  34.7 1.5 %add_convert_fusion.1 = bf16[128,8,512]{2,0,1:T(8,128)(2,1)} fusion(f32[128,8,512]{2,0,1:T(8,128)S(1)} %fusion.32, f32[128,8,512]{2,0,1:T(8,128)S(1)} %fusion.37, bf16[128,576]{0,1:T(8,128)(2,1)S(1)} %copy-done.8, f32[128,8,128]{0,2,1:T(8,128)S(1)} %get-tuple-element.24, f32[128,8]{0,1:T(8,128)S(1)} %add_add_fusion.1, f32[128,8]{0,1:T(8,128)S(1)} %maximum_maximum_fusion), kind=kOutput, calls=%fused_computation.1 | convolution fusion | flops 136183808 | bytes 5906432 | tf_op jit(solution)/shard_map/thk,kc->thc/dot_general | solution.py:97
  36.1 0.7 %convolution_bitcast_fusion.5 = f32[128,512]{0,1:T(8,128)S(1)} fusion(bf16[128,8,512]{2,1,0:T(8,128)(2,1)S(1)} %copy-done.2, f32[128,8,128]{0,2,1:T(8,128)S(1)} %get-tuple-element.22, f32[128,8]{0,1:T(8,128)S(1)} %add_add_fusion.1, f32[128,8]{0,1:T(8,128)S(1)} %maximum_maximum_fusion), kind=kOutput, calls=%fused_computation.13 | convolution fusion | flops 134610944 | bytes 1843200 | tf_op jit(solution)/shard_map/thk,thc->kc/dot_general | solution.py:52
  36.9 1.1 %add_convert_fusion.2 = bf16[128,576]{0,1:T(8,128)(2,1)} fusion(bf16[128,576]{0,1:T(8,128)(2,1)S(1)} %collective-permute-done.3, bf16[128,576]{0,1:T(8,128)(2,1)S(1)} %collective-permute-done.2, f32[128,512]{0,1:T(8,128)S(1)} %convolution_bitcast_fusion.5, bf16[128,8,128]{0,2,1:T(8,128)(2,1)S(1)} %get-tuple-element.17, bf16[128,8,576]{0,2,1:T(8,128)(2,1)S(1)} %copy-done), kind=kOutput, calls=%fused_computation.44 | convolution fusion | flops 151437312 | bytes 2146304 | tf_op jit(solution)/shard_map/thk,thd->kd/dot_general | solution.py:51
  38.0 1.7 %copy.54 = bf16[128,576]{1,0:T(8,128)(2,1)} copy(bf16[128,576]{0,1:T(8,128)(2,1)} %add_convert_fusion.2) | data formatting | bytes 294912 | tf_op jit(solution)/shard_map/convert_element_type | solution.py:123
  39.7 14.1 %all-to-all-start = ((bf16[8,16,576]{2,1,0:T(8,128)(2,1)}), bf16[8,16,576]{2,1,0:T(8,128)(2,1)}, u32[]{:S(2)}, u32[]{:S(2)}) async-start(bf16[8,16,576]{2,1,0:T(8,128)(2,1)} %bitcast.77), calls=%async_computation | async-start | bytes 327680 | tf_op jit(solution)/shard_map/all_to_all | solution.py:28
  53.9 1.6 %fusion.26 = f32[128,8,576]{0,2,1:T(8,128)S(1)} fusion(bf16[128,8,128]{0,2,1:T(8,128)(2,1)} %copy-done.6, bf16[128,576]{0,1:T(8,128)(2,1)} %copy-done.12), kind=kOutput, calls=%fused_computation.48 | convolution fusion | flops 150994944 | bytes 2768896 | tf_op jit(solution)/shard_map/thk,kd->thd/dot_general | solution.py:50
  55.5 1.5 %copy.55 = bf16[128,8,512]{2,1,0:T(8,128)(2,1)} copy(bf16[128,8,512]{2,0,1:T(8,128)(2,1)S(1)} %copy-done.3) | data formatting | bytes 2097152
  57.0 1.6 %add_convert_fusion = bf16[128,8,576]{0,2,1:T(8,128)(2,1)} fusion(f32[128,8,576]{0,2,1:T(8,128)S(1)} %fusion.23, f32[128,8,576]{0,2,1:T(8,128)S(1)} %fusion.26, bf16[128,8,128]{0,2,1:T(8,128)(2,1)S(1)} %copy-done.5, bf16[128,576]{0,1:T(8,128)(2,1)S(1)} %copy-done.9), kind=kOutput, calls=%fused_computation | convolution fusion | flops 152764416 | bytes 6307840 | tf_op jit(solution)/shard_map/thk,kd->thd/dot_general | solution.py:50
  58.6 11.4 %all-to-all-done = bf16[8,16,576]{2,1,0:T(8,128)(2,1)} async-done(((bf16[8,16,576]{2,1,0:T(8,128)(2,1)}), bf16[8,16,576]{2,1,0:T(8,128)(2,1)}, u32[]{:S(2)}, u32[]{:S(2)}) %all-to-all-start) | async-done | bytes 147488 | tf_op jit(solution)/shard_map/all_to_all | solution.py:28
  70.0 1.6 %convert_reduce_fusion = f32[16,576]{1,0:T(8,128)} fusion(bf16[8,16,576]{2,1,0:T(8,128)(2,1)} %all-to-all-done), kind=kLoop, calls=%fused_computation.43 | loop fusion | flops 138240 | bytes 184320 | tf_op jit(solution)/shard_map/reduce_sum | solution.py:29
  (35 shorter events, 0.3 us)
Async XLA Ops:
  0.6 6.8 %copy-start = (bf16[128,8,576]{0,2,1:T(8,128)(2,1)S(1)}, bf16[128,8,576]{0,2,1:T(8,128)(2,1)}, u32[]{:S(2)}) copy-start(bf16[128,8,576]{0,2,1:T(8,128)(2,1)} %param.4) | copy-start | bytes 3538948
  0.6 8.1 %copy-start.10 = (bf16[128,576]{0,1:T(8,128)(2,1)S(1)}, bf16[128,576]{0,1:T(8,128)(2,1)}, u32[]{:S(2)}) copy-start(bf16[128,576]{0,1:T(8,128)(2,1)} %param.5) | copy-start | bytes 442372
  0.7 8.1 %copy-start.1 = (bf16[128,8,512]{2,1,0:T(8,128)(2,1)S(1)}, bf16[128,8,512]{2,1,0:T(8,128)(2,1)}, u32[]{:S(2)}) copy-start(bf16[128,8,512]{2,1,0:T(8,128)(2,1)} %param.7) | copy-start | bytes 3145732
  0.7 20.0 %collective-permute-start.1 = (bf16[128,576]{0,1:T(8,128)(2,1)}, bf16[128,576]{0,1:T(8,128)(2,1)S(1)}, u32[]{:S(2)}, u32[]{:S(2)}) collective-permute-start(bf16[128,576]{0,1:T(8,128)(2,1)} %param.5), channel_id=1, source_target_pairs={{0,8},{8,16},{16,24},{24,32},{32,40},{40,48},{48,56},{56,64},{64,7... | collective-permute-start | bytes 442376 | tf_op jit(solution)/shard_map/ppermute | solution.py:17
  2.7 17.5 %collective-permute-start = (bf16[128,576]{0,1:T(8,128)(2,1)}, bf16[128,576]{0,1:T(8,128)(2,1)S(1)}, u32[]{:S(2)}, u32[]{:S(2)}) collective-permute-start(bf16[128,576]{0,1:T(8,128)(2,1)} %param.5), channel_id=1, source_target_pairs={{0,16},{8,24},{16,32},{24,40},{32,48},{40,56},{48,64},{56,72},{64,... | collective-permute-start | bytes 442376 | tf_op jit(solution)/shard_map/ppermute | solution.py:17
  20.2 3.1 %copy-start.7 = (bf16[128,576]{0,1:T(8,128)(2,1)}, bf16[128,576]{0,1:T(8,128)(2,1)S(1)}, u32[]{:S(2)}) copy-start(bf16[128,576]{0,1:T(8,128)(2,1)S(1)} %collective-permute-done) | copy-start | bytes 442372
  20.7 3.5 %copy-start.12 = (bf16[128,576]{0,1:T(8,128)(2,1)}, bf16[128,576]{0,1:T(8,128)(2,1)S(1)}, u32[]{:S(2)}) copy-start(bf16[128,576]{0,1:T(8,128)(2,1)S(1)} %collective-permute-done.1) | copy-start | bytes 442372
  25.5 5.3 %copy-start.4 = (bf16[128,8,128]{0,2,1:T(8,128)(2,1)}, bf16[128,8,128]{0,2,1:T(8,128)(2,1)S(1)}, u32[]{:S(2)}) copy-start(bf16[128,8,128]{0,2,1:T(8,128)(2,1)S(1)} %get-tuple-element.15) | copy-start | bytes 786436
  25.6 7.3 %copy-start.6 = (bf16[128,8,128]{0,2,1:T(8,128)(2,1)}, bf16[128,8,128]{0,2,1:T(8,128)(2,1)S(1)}, u32[]{:S(2)}) copy-start(bf16[128,8,128]{0,2,1:T(8,128)(2,1)S(1)} %get-tuple-element.16) | copy-start | bytes 786436
  26.0 6.8 %copy-start.11 = (bf16[128,576]{0,1:T(8,128)(2,1)S(1)}, bf16[128,576]{0,1:T(8,128)(2,1)}, u32[]{:S(2)}) copy-start(bf16[128,576]{0,1:T(8,128)(2,1)} %param.5) | copy-start | bytes 442372
  26.1 10.8 %collective-permute-start.3 = (bf16[128,576]{0,1:T(8,128)(2,1)S(1)}, bf16[128,576]{0,1:T(8,128)(2,1)S(1)}, u32[]{:S(2)}, u32[]{:S(2)}) collective-permute-start(bf16[128,576]{0,1:T(8,128)(2,1)S(1)} %fusion.6), channel_id=1, source_target_pairs={{16,0},{24,8},{32,16},{40,24},{48,32},{56,40},{64,48},{72,56},{80,... | collective-permute-start | bytes 442376 | tf_op jit(solution)/shard_map/ppermute | solution.py:17
  30.9 6.0 %collective-permute-start.2 = (bf16[128,576]{0,1:T(8,128)(2,1)S(1)}, bf16[128,576]{0,1:T(8,128)(2,1)S(1)}, u32[]{:S(2)}, u32[]{:S(2)}) collective-permute-start(bf16[128,576]{0,1:T(8,128)(2,1)S(1)} %fusion.7), channel_id=1, source_target_pairs={{8,0},{16,8},{24,16},{32,24},{40,32},{48,40},{56,48},{64,56},{72,6... | collective-permute-start | bytes 442376 | tf_op jit(solution)/shard_map/ppermute | solution.py:17
  32.8 0.9 %copy-start.13 = (bf16[128,576]{0,1:T(8,128)(2,1)S(1)}, bf16[128,576]{0,1:T(8,128)(2,1)}, u32[]{:S(2)}) copy-start(bf16[128,576]{0,1:T(8,128)(2,1)} %copy-done.12) | copy-start | bytes 442372
  33.7 0.9 %copy-start.8 = (bf16[128,576]{0,1:T(8,128)(2,1)S(1)}, bf16[128,576]{0,1:T(8,128)(2,1)}, u32[]{:S(2)}) copy-start(bf16[128,576]{0,1:T(8,128)(2,1)} %copy-done.7) | copy-start | bytes 442372
  34.7 1.5 %copy-start.2 = (bf16[128,8,512]{2,1,0:T(8,128)(2,1)S(1)}, bf16[128,8,512]{2,1,0:T(8,128)(2,1)}, u32[]{:S(2)}) copy-start(bf16[128,8,512]{2,1,0:T(8,128)(2,1)} %param.7) | copy-start | bytes 3145732
  39.7 30.3 %all-to-all-start = ((bf16[8,16,576]{2,1,0:T(8,128)(2,1)}), bf16[8,16,576]{2,1,0:T(8,128)(2,1)}, u32[]{:S(2)}, u32[]{:S(2)}) async-start(bf16[8,16,576]{2,1,0:T(8,128)(2,1)} %bitcast.77), calls=%async_computation | async-start | bytes 327680 | tf_op jit(solution)/shard_map/all_to_all | solution.py:28
  53.9 1.6 %copy-start.3 = (bf16[128,8,512]{2,0,1:T(8,128)(2,1)S(1)}, bf16[128,8,512]{2,0,1:T(8,128)(2,1)}, u32[]{:S(2)}) copy-start(bf16[128,8,512]{2,0,1:T(8,128)(2,1)} %add_convert_fusion.1) | copy-start | bytes 3145732
  55.4 1.6 %copy-start.5 = (bf16[128,8,128]{0,2,1:T(8,128)(2,1)S(1)}, bf16[128,8,128]{0,2,1:T(8,128)(2,1)}, u32[]{:S(2)}) copy-start(bf16[128,8,128]{0,2,1:T(8,128)(2,1)} %copy-done.4) | copy-start | bytes 786436
  55.4 1.6 %copy-start.9 = (bf16[128,576]{0,1:T(8,128)(2,1)S(1)}, bf16[128,576]{0,1:T(8,128)(2,1)}, u32[]{:S(2)}) copy-start(bf16[128,576]{0,1:T(8,128)(2,1)} %copy-done.7) | copy-start | bytes 442372
where the time goes:
time: 72 us; the launch traced here: 71.6 us
  starting transfers between devices  26.3 us (37%)
  waiting for transfers between devices  22.1 us (31%)
  matrix products  15 us (21%)
  local copies, waits for them, and re-layouts  4.2 us (6%)
  other arithmetic  3.03 us (4%)
  between operations  1 us (1%)
    all_to_all x1, starting transfers between devices, sent_and_summed(): pieces = lax.all_to_all(in_blocks(x, dim, devices), axis, 0, 0, tiled=True)  14.1 us
    ppermute x4, starting transfers between devices, shifted(): lax.ppermute(value, axis, [(source, source + steps) for source in range(l...  12.1 us
    all_to_all x1, waiting for transfers between devices, sent_and_summed(): pieces = lax.all_to_all(in_blocks(x, dim, devices), axis, 0, 0, tiled=True)  11.4 us
    ppermute x4, waiting for transfers between devices, shifted(): lax.ppermute(value, axis, [(source, source + steps) for source in range(l...  10.7 us
    dot_general x3, matrix products, block_grads(): jnp.einsum('thk,kd->thd', dscore, key_block, preferred_element_type=jnp.f...  3.64 us
    dot_general x3, matrix products, value_product(): jnp.einsum('thc,kc->thk', out_grad, key_block[:, :latent_width], preferre...  2.51 us
    unnamed x29, local copies, waits for them, and re-layouts  2.49 us
    dot_general x3, matrix products, shards(): jnp.einsum('thk,kc->thc', weights, key_block[:, :latent_width], preferred...  2.4 us
  transfers between devices with their start and end apart: 5, of which 2 were waited for; matrix products, arithmetic and copies ran while one was open for 16% of the time, Pallas kernels for 0%

commit v1 on v0

v1 whole, which is shorter than its diff:
```python
import jax
import jax.numpy as jnp
from jax import lax
from jax.experimental import pallas as pl
from jax.experimental.pallas import tpu as pltpu
from jax.sharding import PartitionSpec as P

MAXDOC = 256
SCALE = 192 ** (-0.5)
BF = jnp.bfloat16
F32 = jnp.float32
NT = (((1,), (1,)), ((), ()))
NN = (((1,), (0,)), ((), ()))
TN = (((0,), (0,)), ((), ()))


def dot(a, b, dims):
    return lax.dot_general(a, b, dims, preferred_element_type=F32)


def own_kernel(q_ref, g_ref, k_ref, gh_ref, s_ref, p_ref, wide):
    heads, lat = g_ref.shape[1], g_ref.shape[2]
    tok = g_ref.shape[0]
    for c in range(lat // 128):
        wide[c] = g_ref[:, :, c * 128 : (c + 1) * 128].astype(F32).reshape(tok * heads, 128)
    keys = k_ref[...].T
    for h in range(0, heads, 2):
        for i in (h, h + 1):
            for c in range(lat // 128):
                part = wide[c, pl.ds(i, tok, stride=heads), :]
                gh_ref[i * tok : (i + 1) * tok, c * 128 : (c + 1) * 128] = part.astype(BF)
        cols = slice(h * tok, (h + 2) * tok)
        qs = jnp.concatenate([q_ref[h], q_ref[h + 1]], axis=1)
        s_ref[:, cols] = dot(keys, qs, NN)
        p_ref[:, cols] = dot(keys[:, :lat], gh_ref[cols, :], NT)


def main_kernel(ctx_ref, q_ref, gh_ref, s_ref, p_ref, k2_ref, k1_ref, doc_ref, w_ref, ds_ref, a2_ref, a1_ref):
    heads = q_ref.shape[0]
    tok = q_ref.shape[2]
    lat = gh_ref.shape[1]
    keys = jnp.concatenate([k2_ref[...].T, k1_ref[...].T], axis=0)
    base = ctx_ref[0] * tok
    kpos = base - 2 * tok + lax.broadcasted_iota(jnp.int32, (3 * tok, 2 * tok), 0)
    qpos = base + (lax.broadcasted_iota(jnp.int32, (3 * tok, 2 * tok), 1) % tok)
    doc = jnp.concatenate([doc_ref[...], doc_ref[...]], axis=1)
    seen = (kpos >= doc) & (kpos <= qpos)
    for h in range(0, heads, 2):
        cols = slice(h * tok, (h + 2) * tok)
        qs = jnp.concatenate([q_ref[h], q_ref[h + 1]], axis=1)
        s = jnp.concatenate([dot(keys, qs, NN), s_ref[:, cols]], axis=0) * SCALE
        s = jnp.where(seen, s, -jnp.inf)
        top = jnp.max(s, axis=0, keepdims=True)
        e = jnp.exp(s - top)
        prob = e * (1.0 / jnp.sum(e, axis=0, keepdims=True))
        dp = jnp.concatenate([dot(keys[:, :lat], gh_ref[cols, :], NT), p_ref[:, cols]], axis=0)
        delta = jnp.sum(prob * dp, axis=0, keepdims=True)
        w_ref[:, cols] = prob.astype(BF)
        ds_ref[:, cols] = (SCALE * prob * (dp - delta)).astype(BF)
    partial_grad(w_ref, ds_ref, q_ref, gh_ref, 0, a2_ref)
    partial_grad(w_ref, ds_ref, q_ref, gh_ref, 1, a1_ref)


def partial_grad(w_ref, ds_ref, q_ref, gh_ref, block, out_ref):
    heads, _, tok = q_ref.shape
    lat = gh_ref.shape[1]
    rows = slice(block * tok, (block + 1) * tok)
    qs = jnp.concatenate([q_ref[h] for h in range(heads)], axis=1)
    score_part = dot(ds_ref[rows, :], qs, NT)
    value_part = dot(w_ref[rows, :], gh_ref[...], NN)
    out_ref[:, :lat] = (score_part[:, :lat] + value_part).astype(out_ref.dtype)
    out_ref[:, lat:] = score_part[:, lat:].astype(out_ref.dtype)


def last_kernel(w_ref, ds_ref, q_ref, gh_ref, o_ref):
    partial_grad(w_ref, ds_ref, q_ref, gh_ref, 2, o_ref)


def out_kernel(w_ref, ds_ref, k2_ref, k1_ref, k0_ref, att_ref, dq_ref, wide):
    heads = dq_ref.shape[0]
    tok = dq_ref.shape[2]
    lat = att_ref.shape[2]
    kt = jnp.concatenate([k2_ref[...], k1_ref[...], k0_ref[...]], axis=1)
    for h in range(0, heads, 2):
        cols = slice(h * tok, (h + 2) * tok)
        dq = dot(kt, ds_ref[:, cols], NN).astype(BF)
        dq_ref[h] = dq[:, :tok]
        dq_ref[h + 1] = dq[:, tok:]
        for i in (h, h + 1):
            att = dot(w_ref[:, i * tok : (i + 1) * tok].T, kt[:lat, :], NT)
            for c in range(lat // 128):
                wide[c, pl.ds(i, tok, stride=heads), :] = att[:, c * 128 : (c + 1) * 128]
    for c in range(lat // 128):
        att_ref[:, :, c * 128 : (c + 1) * 128] = wide[c].reshape(tok, heads, 128).astype(BF)


def ctx_pairs(step, ctx_count, head_count, row):
    pairs = []
    for source in range(ctx_count):
        target = source + step
        if 0 <= target < ctx_count:
            flip = source // row != target // row
            for head in range(head_count):
                pairs.append((source * head_count + head, target * head_count + (head ^ 1 if flip else head)))
    return pairs


def shards(query_heads, key_latent, doc_start, out_grad):
    tok, heads, width = query_heads.shape
    lat = out_grad.shape[2]
    ctx_count = lax.axis_size("ctx")
    head_count = lax.axis_size("head")
    both = ("ctx", "head")
    rows = tok * heads

    def shift(value, step):
        return lax.ppermute(value, both, ctx_pairs(step, ctx_count, head_count, 16))

    ctx_index = lax.axis_index("ctx").astype(jnp.int32)
    k2 = shift(key_latent, 2).T
    k1 = shift(key_latent, 1).T
    k0 = key_latent.T
    qt = jnp.transpose(query_heads, (1, 2, 0))
    vmem = pl.BlockSpec(memory_space=pltpu.VMEM)
    smem = pl.BlockSpec(memory_space=pltpu.SMEM)
    shape = jax.ShapeDtypeStruct
    gh, s0, p0 = pl.pallas_call(
        own_kernel,
        out_shape=(shape((rows, lat), BF), shape((tok, rows), F32), shape((tok, rows), F32)),
        in_specs=[vmem] * 3,
        out_specs=(vmem,) * 3,
        scratch_shapes=[pltpu.VMEM((lat // 128, rows, 128), F32)],
        name="own",
    )(qt, out_grad, k0)
    w, ds, a2, a1 = pl.pallas_call(
        main_kernel,
        out_shape=(
            shape((3 * tok, rows), BF),
            shape((3 * tok, rows), BF),
            shape((tok, width), BF),
            shape((tok, width), BF),
        ),
        in_specs=[smem] + [vmem] * 7,
        out_specs=(vmem,) * 4,
        name="main",
    )(ctx_index.reshape(1), qt, gh, s0, p0, k2, k1, doc_start.reshape(1, tok))
    r2 = shift(a2, -2)
    r1 = shift(a1, -1)
    own = pl.pallas_call(
        last_kernel, out_shape=shape((tok, width), F32), in_specs=[vmem] * 4, out_specs=vmem, name="last"
    )(w, ds, qt, gh)
    att, dq = pl.pallas_call(
        out_kernel,
        out_shape=(shape((tok, heads, lat), BF), shape((heads, width, tok), BF)),
        in_specs=[vmem] * 5,
        out_specs=(vmem,) * 2,
        scratch_shapes=[pltpu.VMEM((lat // 128, rows, 128), F32)],
        name="outs",
    )(w, ds, k2, k1, k0)
    owned = (own + r2.astype(F32) + r1.astype(F32)).astype(BF)
    fours = head_count // 2
    groups = [[2 * y + z for y in range(fours)] for z in range(2)]
    pieces = lax.all_to_all(
        owned.reshape(fours, tok // fours, width), "head", 0, 0, axis_index_groups=groups, tiled=True
    )
    halves = jnp.sum(pieces.astype(F32), axis=0).reshape(2, tok // head_count, width)
    z = lax.axis_index("head") % 2
    mine = jnp.where(z == 0, halves[0], halves[1])
    other = jnp.where(z == 0, halves[1], halves[0]).astype(BF)
    got = lax.ppermute(other, "head", [(i, i ^ 1) for i in range(head_count)])
    d_key = mine + got.astype(F32)
    return (att, jnp.transpose(dq, (2, 0, 1)), d_key)


def solution(mesh):
    return jax.shard_map(
        shards,
        mesh=mesh,
        in_specs=(P("ctx", "head", None), P("ctx", None), P("ctx"), P("ctx", "head", None)),
        out_specs=(P("ctx", "head", None), P("ctx", "head", None), P(("ctx", "head"), None)),
        check_vma=False,
    )
```

time: 72 us -> 62.4 us (0.87)
  Pallas kernels: 0 us -> 16.9 us
  matrix products: 15 us -> 0 us
  waiting for transfers between devices: 22.1 us -> 14.9 us
  local copies, waits for them, and re-layouts: 4.2 us -> 0.65 us
    pallas_call x0 -> x4, Pallas kernels: none -> 16.9 us  [the longest x1 5.18 us: shards(): pl.pallas_call(main_kernel, out_shape=(shape((3 * tok, rows), BF), shape(...]
    dot_general x18 -> x0, matrix products: 15 us -> none  [the longest x3 3.64 us: block_grads(): jnp.einsum('thk,kd->thd', dscore, key_block, preferred_element_type=jnp.f...]
    ppermute x4 -> x5, starting transfers between devices: 12.1 us -> 21.9 us  [the longest x4 12.7 us: shift(): return lax.ppermute(value, both, ctx_pairs(step, ctx_count, head_count, 16))]
    all_to_all x1, starting transfers between devices: 14.1 us -> 4.47 us  [shards(): lax.all_to_all(owned.reshape(fours, tok // fours, width), 'head', 0, 0, a...]
    all_to_all x1, waiting for transfers between devices: 11.4 us -> 6.15 us  [shards(): lax.all_to_all(owned.reshape(fours, tok // fours, width), 'head', 0, 0, a...]
    ppermute x4 -> x5, waiting for transfers between devices: 10.7 us -> 8.8 us  [the longest x4 8.07 us: shift(): return lax.ppermute(value, both, ctx_pairs(step, ctx_count, head_count, 16))]
    unnamed x29 -> x4, local copies, waits for them, and re-layouts: 2.49 us -> 0.65 us
    reduce_sum x2 -> x1, other arithmetic: 1.8 us -> 0.03 us  [shards(): jnp.sum(pieces.astype(F32), axis=0).reshape(2, tok // head_count, width)]
  transfers between devices with their start and end apart: 5 -> 6, of which waited for: 2 -> 4; matrix products, arithmetic and copies ran while one was open for 16% -> 0% of each run, Pallas kernels for 0% -> 19%
where the time goes in v1:
time: 62.4 us; the launch traced here: 61.9 us
  starting transfers between devices  26.4 us (42%)
  Pallas kernels  16.9 us (27%)
  waiting for transfers between devices  14.9 us (24%)
  other arithmetic  2.35 us (4%)
  between operations  0.69 us (1%)
  local copies, waits for them, and re-layouts  0.65 us (1%)
    ppermute x4, starting transfers between devices, shift(): return lax.ppermute(value, both, ctx_pairs(step, ctx_count, head_count, 16))  12.7 us
    ppermute x1, starting transfers between devices, shards(): got = lax.ppermute(other, 'head', [(i, i ^ 1) for i in range(head_count)])  9.21 us
    ppermute x4, waiting for transfers between devices, shift(): return lax.ppermute(value, both, ctx_pairs(step, ctx_count, head_count, 16))  8.07 us
    all_to_all x1, waiting for transfers between devices, shards(): lax.all_to_all(owned.reshape(fours, tok // fours, width), 'head', 0, 0, a...  6.15 us
    pallas_call x1, Pallas kernels, shards(): pl.pallas_call(main_kernel, out_shape=(shape((3 * tok, rows), BF), shape(...  5.18 us
    all_to_all x1, starting transfers between devices, shards(): lax.all_to_all(owned.reshape(fours, tok // fours, width), 'head', 0, 0, a...  4.47 us
    pallas_call x1, Pallas kernels, shards(): pl.pallas_call(out_kernel, out_shape=(shape((tok, heads, lat), BF), shape...  4.44 us
    pallas_call x1, Pallas kernels, shards(): pl.pallas_call(own_kernel, out_shape=(shape((rows, lat), BF), shape((tok,...  3.82 us
  transfers between devices with their start and end apart: 6, of which 4 were waited for; matrix products, arithmetic and copies ran while one was open for 0% of the time, Pallas kernels for 19%

profile of v1, /device:TPU:6, one launch (start us, length us, event | category | flops | bytes accessed | tf_op | source)
XLA Modules:
  0.0 61.9 jit_solution(13817283256857776702)
XLA Ops:
  0.6 1.9 %collective-permute-start.1 = (bf16[128,576]{0,1:T(8,128)(2,1)}, bf16[128,576]{0,1:T(8,128)(2,1)S(1)}, u32[]{:S(2)}, u32[]{:S(2)}) collective-permute-start(bf16[128,576]{0,1:T(8,128)(2,1)} %param.5), channel_id=1, source_target_pairs={{0,8},{1,9},{2,10},{3,11},{4,12},{5,13},{6,14},{7,15},{8,16},{9,17... | collective-permute-start | bytes 442376 | tf_op jit(solution)/shard_map/ppermute | solution.py:117
  2.6 3.8 %collective-permute-start = (bf16[128,576]{0,1:T(8,128)(2,1)}, bf16[128,576]{0,1:T(8,128)(2,1)S(1)}, u32[]{:S(2)}, u32[]{:S(2)}) collective-permute-start(bf16[128,576]{0,1:T(8,128)(2,1)} %param.5), channel_id=1, source_target_pairs={{0,16},{1,17},{2,18},{3,19},{4,20},{5,21},{6,22},{7,23},{8,24},{9,... | collective-permute-start | bytes 442376 | tf_op jit(solution)/shard_map/ppermute | solution.py:117
  6.4 3.8 %own.1 = (bf16[1024,512]{1,0:T(8,128)(2,1)}, f32[128,1024]{1,0:T(8,128)}, f32[128,1024]{1,0:T(8,128)}) custom-call(bf16[8,576,128]{2,1,0:T(8,128)(2,1)} %bitcast.8, bf16[128,8,512]{2,1,0:T(8,128)(2,1)} %g_ref.1, bf16[576,128]{1,0:T(8,128)(2,1)} %bitcast.11), custom_call_target="tpu_custom_call" | custom-call | tf_op jit(solution)/shard_map/own/pallas_call | solution.py:127
  10.2 4.6 %collective-permute-done.1 = bf16[128,576]{0,1:T(8,128)(2,1)S(1)} collective-permute-done((bf16[128,576]{0,1:T(8,128)(2,1)}, bf16[128,576]{0,1:T(8,128)(2,1)S(1)}, u32[]{:S(2)}, u32[]{:S(2)}) %collective-permute-start.1) | collective-permute-done | bytes 147488 | tf_op jit(solution)/shard_map/ppermute | solution.py:117
  14.8 0.0 copy-start
  14.8 3.5 %collective-permute-done = bf16[128,576]{0,1:T(8,128)(2,1)S(1)} collective-permute-done((bf16[128,576]{0,1:T(8,128)(2,1)}, bf16[128,576]{0,1:T(8,128)(2,1)S(1)}, u32[]{:S(2)}, u32[]{:S(2)}) %collective-permute-start) | collective-permute-done | bytes 147488 | tf_op jit(solution)/shard_map/ppermute | solution.py:117
  18.3 0.0 copy-start.1
  18.3 0.0 copy-done
  18.3 0.6 %copy-done.1 = bf16[128,576]{0,1:T(8,128)(2,1)} copy-done((bf16[128,576]{0,1:T(8,128)(2,1)}, bf16[128,576]{0,1:T(8,128)(2,1)S(1)}, u32[]{:S(2)}) %copy-start.1) | copy-done | bytes 147480
  18.9 5.2 %main.1 = (bf16[384,1024]{1,0:T(8,128)(2,1)}, bf16[384,1024]{1,0:T(8,128)(2,1)}, bf16[128,576]{1,0:T(8,128)(2,1)}, bf16[128,576]{1,0:T(8,128)(2,1)}) custom-call(s32[1]{0:T(128)} %bitcast.ctx_ref, bf16[8,576,128]{2,1,0:T(8,128)(2,1)} %bitcast.9, bf16[1024,512]{1,0:T(8,128)(2,1)} %get-tuple-element.12.gh_ref, f32[128,1024]{1,0:T(8,128)} %get-tuple-element.13.s_ref, ...), custom_call_target="tpu_custom_call" | custom-call | tf_op jit(solution)/shard_map/main/pallas_call | solution.py:135
  24.1 4.2 %collective-permute-start.2 = (bf16[128,576]{1,0:T(8,128)(2,1)}, bf16[128,576]{1,0:T(8,128)(2,1)S(1)}, u32[]{:S(2)}, u32[]{:S(2)}) collective-permute-start(bf16[128,576]{1,0:T(8,128)(2,1)} %get-tuple-element.19), channel_id=1, source_target_pairs={{16,0},{17,1},{18,2},{19,3},{20,4},{21,5},{22,6},{23,7},{24,8},{25... | collective-permute-start | bytes 442376 | tf_op jit(solution)/shard_map/ppermute | solution.py:117
  28.3 2.8 %collective-permute-start.3 = (bf16[128,576]{1,0:T(8,128)(2,1)}, bf16[128,576]{1,0:T(8,128)(2,1)S(1)}, u32[]{:S(2)}, u32[]{:S(2)}) collective-permute-start(bf16[128,576]{1,0:T(8,128)(2,1)} %get-tuple-element.20), channel_id=1, source_target_pairs={{8,0},{9,1},{10,2},{11,3},{12,4},{13,5},{14,6},{15,7},{16,8},{17,9... | collective-permute-start | bytes 442376 | tf_op jit(solution)/shard_map/ppermute | solution.py:117
  31.1 3.5 %last.1 = f32[128,576]{1,0:T(8,128)} custom-call(bf16[384,1024]{1,0:T(8,128)(2,1)} %get-tuple-element.15.w_ref, bf16[384,1024]{1,0:T(8,128)(2,1)} %get-tuple-element.16.ds_ref, bf16[8,576,128]{2,1,0:T(8,128)(2,1)} %bitcast.10, bf16[1024,512]{1,0:T(8,128)(2,1)} %get-tuple-element.12.gh_ref), custom_call_target="tpu_custom_call" | custom-call | tf_op jit(solution)/shard_map/last/pallas_call | solution.py:149
  34.6 0.0 collective-permute-done.2
  34.6 0.0 collective-permute-done.3
  34.6 1.7 %add_convert_fusion = bf16[128,576]{1,0:T(8,128)(2,1)} fusion(bf16[128,576]{1,0:T(8,128)(2,1)S(1)} %collective-permute-done.3, f32[128,576]{1,0:T(8,128)} %last.1, bf16[128,576]{1,0:T(8,128)(2,1)S(1)} %collective-permute-done.2), kind=kLoop, calls=%fused_computation.1 | loop fusion | flops 368640 | bytes 737280 | tf_op jit(solution)/shard_map/convert_element_type | solution.py:160
  36.3 4.5 %all-to-all-start = ((bf16[4,32,576]{2,1,0:T(8,128)(2,1)}), bf16[4,32,576]{2,1,0:T(8,128)(2,1)S(1)}, u32[]{:S(2)}, u32[]{:S(2)}) async-start(bf16[4,32,576]{2,1,0:T(8,128)(2,1)} %bitcast.7), calls=%async_computation | async-start | bytes 327680 | tf_op jit(solution)/shard_map/all_to_all | solution.py:163
  40.7 6.2 %all-to-all-done = bf16[4,32,576]{2,1,0:T(8,128)(2,1)S(1)} async-done(((bf16[4,32,576]{2,1,0:T(8,128)(2,1)}), bf16[4,32,576]{2,1,0:T(8,128)(2,1)S(1)}, u32[]{:S(2)}, u32[]{:S(2)}) %all-to-all-start) | async-done | bytes 147488 | tf_op jit(solution)/shard_map/all_to_all | solution.py:163
  46.9 9.2 %collective-permute-start.4 = (bf16[16,576]{1,0:T(8,128)(2,1)S(1)}, bf16[16,576]{1,0:T(8,128)(2,1)S(1)}, u32[]{:S(2)}, u32[]{:S(2)}) collective-permute-start(bf16[16,576]{1,0:T(8,128)(2,1)S(1)} %select_convert_fusion), channel_id=1, source_target_pairs={{0,1},{1,0},{2,3},{3,2},{4,5},{5,4},{6,7},{7,6},{8,9},{9,8},{10,11... | collective-permute-start | bytes 55304 | tf_op jit(solution)/shard_map/ppermute | solution.py:170
  56.1 4.4 %outs.1 = (bf16[128,8,512]{2,1,0:T(8,128)(2,1)}, bf16[8,576,128]{2,1,0:T(8,128)(2,1)}) custom-call(bf16[384,1024]{1,0:T(8,128)(2,1)} %get-tuple-element.15.w_ref, bf16[384,1024]{1,0:T(8,128)(2,1)} %get-tuple-element.16.ds_ref, bf16[576,128]{1,0:T(8,128)(2,1)} %bitcast.16, bf16[576,128]{1,0:T(8,128)(2,1)} %bitcast.14, bf16[576,128]{1,0:T(8,128)(2,1)} %bitcast.12), custom_call_target="tpu_custom_call" | custom-call | tf_op jit(solution)/shard_map/outs/pallas_call | solution.py:152
  60.6 0.7 %collective-permute-done.4 = bf16[16,576]{1,0:T(8,128)(2,1)S(1)} collective-permute-done((bf16[16,576]{1,0:T(8,128)(2,1)S(1)}, bf16[16,576]{1,0:T(8,128)(2,1)S(1)}, u32[]{:S(2)}, u32[]{:S(2)}) %collective-permute-start.4) | collective-permute-done | bytes 18464 | tf_op jit(solution)/shard_map/ppermute | solution.py:170
  61.3 0.6 %convert_add_fusion = f32[16,576]{1,0:T(8,128)} fusion(bf16[16,576]{1,0:T(8,128)(2,1)S(1)} %collective-permute-done.4, f32[32,576]{1,0:T(8,128)S(1)} %convert_reduce_fusion, pred[]{:T(512)S(6)} %eq.6), kind=kLoop, calls=%fused_computation.2 | loop fusion | flops 27648 | bytes 129025 | tf_op jit(solution)/shard_map/add | solution.py:171
  (2 shorter events, 0.0 us)
Async XLA Ops:
  0.6 14.1 %collective-permute-start.1 = (bf16[128,576]{0,1:T(8,128)(2,1)}, bf16[128,576]{0,1:T(8,128)(2,1)S(1)}, u32[]{:S(2)}, u32[]{:S(2)}) collective-permute-start(bf16[128,576]{0,1:T(8,128)(2,1)} %param.5), channel_id=1, source_target_pairs={{0,8},{1,9},{2,10},{3,11},{4,12},{5,13},{6,14},{7,15},{8,16},{9,17... | collective-permute-start | bytes 442376 | tf_op jit(solution)/shard_map/ppermute | solution.py:117
  2.6 15.7 %collective-permute-start = (bf16[128,576]{0,1:T(8,128)(2,1)}, bf16[128,576]{0,1:T(8,128)(2,1)S(1)}, u32[]{:S(2)}, u32[]{:S(2)}) collective-permute-start(bf16[128,576]{0,1:T(8,128)(2,1)} %param.5), channel_id=1, source_target_pairs={{0,16},{1,17},{2,18},{3,19},{4,20},{5,21},{6,22},{7,23},{8,24},{9,... | collective-permute-start | bytes 442376 | tf_op jit(solution)/shard_map/ppermute | solution.py:117
  14.8 3.5 %copy-start = (bf16[128,576]{0,1:T(8,128)(2,1)}, bf16[128,576]{0,1:T(8,128)(2,1)S(1)}, u32[]{:S(2)}) copy-start(bf16[128,576]{0,1:T(8,128)(2,1)S(1)} %collective-permute-done.1) | copy-start | bytes 442372
  18.3 0.7 %copy-start.1 = (bf16[128,576]{0,1:T(8,128)(2,1)}, bf16[128,576]{0,1:T(8,128)(2,1)S(1)}, u32[]{:S(2)}) copy-start(bf16[128,576]{0,1:T(8,128)(2,1)S(1)} %collective-permute-done) | copy-start | bytes 442372
  24.1 10.4 %collective-permute-start.2 = (bf16[128,576]{1,0:T(8,128)(2,1)}, bf16[128,576]{1,0:T(8,128)(2,1)S(1)}, u32[]{:S(2)}, u32[]{:S(2)}) collective-permute-start(bf16[128,576]{1,0:T(8,128)(2,1)} %get-tuple-element.19), channel_id=1, source_target_pairs={{16,0},{17,1},{18,2},{19,3},{20,4},{21,5},{22,6},{23,7},{24,8},{25... | collective-permute-start | bytes 442376 | tf_op jit(solution)/shard_map/ppermute | solution.py:117
  28.3 6.3 %collective-permute-start.3 = (bf16[128,576]{1,0:T(8,128)(2,1)}, bf16[128,576]{1,0:T(8,128)(2,1)S(1)}, u32[]{:S(2)}, u32[]{:S(2)}) collective-permute-start(bf16[128,576]{1,0:T(8,128)(2,1)} %get-tuple-element.20), channel_id=1, source_target_pairs={{8,0},{9,1},{10,2},{11,3},{12,4},{13,5},{14,6},{15,7},{16,8},{17,9... | collective-permute-start | bytes 442376 | tf_op jit(solution)/shard_map/ppermute | solution.py:117
  36.3 10.6 %all-to-all-start = ((bf16[4,32,576]{2,1,0:T(8,128)(2,1)}), bf16[4,32,576]{2,1,0:T(8,128)(2,1)S(1)}, u32[]{:S(2)}, u32[]{:S(2)}) async-start(bf16[4,32,576]{2,1,0:T(8,128)(2,1)} %bitcast.7), calls=%async_computation | async-start | bytes 327680 | tf_op jit(solution)/shard_map/all_to_all | solution.py:163
  46.9 14.4 %collective-permute-start.4 = (bf16[16,576]{1,0:T(8,128)(2,1)S(1)}, bf16[16,576]{1,0:T(8,128)(2,1)S(1)}, u32[]{:S(2)}, u32[]{:S(2)}) collective-permute-start(bf16[16,576]{1,0:T(8,128)(2,1)S(1)} %select_convert_fusion), channel_id=1, source_target_pairs={{0,1},{1,0},{2,3},{3,2},{4,5},{5,4},{6,7},{7,6},{8,9},{9,8},{10,11... | collective-permute-start | bytes 55304 | tf_op jit(solution)/shard_map/ppermute | solution.py:170

commit v2 on v1

v2 whole, which is shorter than its diff:
```python
import jax
import jax.numpy as jnp
from jax import lax
from jax.experimental import pallas as pl
from jax.experimental.pallas import tpu as pltpu
from jax.sharding import PartitionSpec as P

SCALE = 192 ** (-0.5)
BF = jnp.bfloat16
F32 = jnp.float32
NT = (((1,), (1,)), ((), ()))
NN = (((1,), (0,)), ((), ()))


def dot(a, b, dims):
    return lax.dot_general(a, b, dims, preferred_element_type=F32)


def own_kernel(q_ref, g_ref, k_ref, qv_ref, kv_ref, gh_ref, s_ref, p_ref, gbuf, wide, sems):
    heads, _, tok = qv_ref.shape
    lat = gh_ref.shape[1]
    parts = 4
    size = tok // parts
    g_copies = []
    for n in range(parts):
        piece = slice(n * size, (n + 1) * size)
        g_copies.append(pltpu.make_async_copy(g_ref.at[piece], gbuf.at[piece], sems.at[n]))
    q_copies = [pltpu.make_async_copy(q_ref.at[h], qv_ref.at[h], sems.at[parts + h]) for h in range(heads)]
    k_copy = pltpu.make_async_copy(k_ref, kv_ref, sems.at[parts + heads])
    for copy in [k_copy] + g_copies + q_copies:
        copy.start()
    k_copy.wait()
    keys = kv_ref[...].T
    for n in range(parts):
        g_copies[n].wait()
        piece = slice(n * size, (n + 1) * size)
        rows = slice(n * size * heads, (n + 1) * size * heads)
        for c in range(lat // 128):
            wide[c, rows, :] = gbuf[piece, :, c * 128 : (c + 1) * 128].astype(F32).reshape(size * heads, 128)
    for h in range(0, heads, 2):
        for i in (h, h + 1):
            for c in range(lat // 128):
                part = wide[c, pl.ds(i, tok, stride=heads), :]
                gh_ref[i * tok : (i + 1) * tok, c * 128 : (c + 1) * 128] = part.astype(BF)
            q_copies[i].wait()
        cols = slice(h * tok, (h + 2) * tok)
        qs = jnp.concatenate([qv_ref[h], qv_ref[h + 1]], axis=1)
        s_ref[:, cols] = dot(keys, qs, NN)
        p_ref[:, cols] = dot(keys[:, :lat], gh_ref[cols, :], NT)


def mid_kernel(q_ref, gh_ref, k_ref, s_ref, p_ref):
    heads, _, tok = q_ref.shape
    lat = gh_ref.shape[1]
    keys = k_ref[...].T
    for h in range(0, heads, 2):
        cols = slice(h * tok, (h + 2) * tok)
        qs = jnp.concatenate([q_ref[h], q_ref[h + 1]], axis=1)
        s_ref[:, cols] = dot(keys, qs, NN)
        p_ref[:, cols] = dot(keys[:, :lat], gh_ref[cols, :], NT)


def main_kernel(ctx_ref, q_ref, gh_ref, s0_ref, p0_ref, s1_ref, p1_ref, k2_ref, doc_ref, w_ref, ds_ref, a2_ref):
    heads, _, tok = q_ref.shape
    lat = gh_ref.shape[1]
    keys = k2_ref[...].T
    base = ctx_ref[0] * tok
    kpos = base - 2 * tok + lax.broadcasted_iota(jnp.int32, (3 * tok, 2 * tok), 0)
    qpos = base + (lax.broadcasted_iota(jnp.int32, (3 * tok, 2 * tok), 1) % tok)
    doc = jnp.concatenate([doc_ref[...], doc_ref[...]], axis=1)
    seen = (kpos >= doc) & (kpos <= qpos)
    for h in range(0, heads, 2):
        cols = slice(h * tok, (h + 2) * tok)
        qs = jnp.concatenate([q_ref[h], q_ref[h + 1]], axis=1)
        s = jnp.concatenate([dot(keys, qs, NN), s1_ref[:, cols], s0_ref[:, cols]], axis=0) * SCALE
        s = jnp.where(seen, s, -jnp.inf)
        top = jnp.max(s, axis=0, keepdims=True)
        e = jnp.exp(s - top)
        prob = e * (1.0 / jnp.sum(e, axis=0, keepdims=True))
        dp = jnp.concatenate([dot(keys[:, :lat], gh_ref[cols, :], NT), p1_ref[:, cols], p0_ref[:, cols]], axis=0)
        delta = jnp.sum(prob * dp, axis=0, keepdims=True)
        w_ref[:, cols] = prob.astype(BF)
        ds_ref[:, cols] = (SCALE * prob * (dp - delta)).astype(BF)
    partial_grad(w_ref, ds_ref, q_ref, gh_ref, 0, a2_ref)


def partial_grad(w_ref, ds_ref, q_ref, gh_ref, block, out_ref):
    heads, _, tok = q_ref.shape
    lat = gh_ref.shape[1]
    rows = slice(block * tok, (block + 1) * tok)
    qs = jnp.concatenate([q_ref[h] for h in range(heads)], axis=1)
    score_part = dot(ds_ref[rows, :], qs, NT)
    value_part = dot(w_ref[rows, :], gh_ref[...], NN)
    out_ref[:, :lat] = (score_part[:, :lat] + value_part).astype(out_ref.dtype)
    out_ref[:, lat:] = score_part[:, lat:].astype(out_ref.dtype)


def back_kernel(w_ref, ds_ref, q_ref, gh_ref, o_ref):
    partial_grad(w_ref, ds_ref, q_ref, gh_ref, 1, o_ref)


def last_kernel(w_ref, ds_ref, q_ref, gh_ref, o_ref):
    partial_grad(w_ref, ds_ref, q_ref, gh_ref, 2, o_ref)


def add_kernel(own_ref, r2_ref, r1_ref, o_ref):
    total = own_ref[...] + r2_ref[...].astype(F32) + r1_ref[...].astype(F32)
    o_ref[...] = total.reshape(o_ref.shape).astype(BF)


def out_kernel(w_ref, ds_ref, k2_ref, k1_ref, k0_ref, att_ref, dq_ref, wide):
    heads = dq_ref.shape[0]
    tok = dq_ref.shape[2]
    lat = att_ref.shape[2]
    kt = jnp.concatenate([k2_ref[...], k1_ref[...], k0_ref[...]], axis=1)
    for h in range(0, heads, 2):
        cols = slice(h * tok, (h + 2) * tok)
        dq = dot(kt, ds_ref[:, cols], NN).astype(BF)
        dq_ref[h] = dq[:, :tok]
        dq_ref[h + 1] = dq[:, tok:]
        for i in (h, h + 1):
            att = dot(w_ref[:, i * tok : (i + 1) * tok].T, kt[:lat, :], NT)
            for c in range(lat // 128):
                wide[c, pl.ds(i, tok, stride=heads), :] = att[:, c * 128 : (c + 1) * 128]
    for c in range(lat // 128):
        att_ref[:, :, c * 128 : (c + 1) * 128] = wide[c].reshape(tok, heads, 128).astype(BF)


def ctx_pairs(step, ctx_count, head_count, row):
    pairs = []
    for source in range(ctx_count):
        target = source + step
        if 0 <= target < ctx_count:
            flip = source // row != target // row
            for head in range(head_count):
                pairs.append((source * head_count + head, target * head_count + (head ^ 1 if flip else head)))
    return pairs


def step(query_heads, key_latent, doc_start, out_grad):
    tok, heads, width = query_heads.shape
    lat = out_grad.shape[2]
    ctx_count = lax.axis_size("ctx")
    head_count = lax.axis_size("head")
    both = ("ctx", "head")
    rows = tok * heads

    def shift(value, step):
        return lax.ppermute(value, both, ctx_pairs(step, ctx_count, head_count, 16))

    ctx_index = lax.axis_index("ctx").astype(jnp.int32)
    k2 = shift(key_latent, 2).T
    k1 = shift(key_latent, 1).T
    k0 = key_latent.T
    qt = jnp.transpose(query_heads, (1, 2, 0))
    k2, k1 = (pltpu.with_memory_space_constraint(x, pltpu.VMEM) for x in (k2, k1))
    qt, out_grad, k0 = (pltpu.with_memory_space_constraint(x, pltpu.HBM) for x in (qt, out_grad, k0))
    vmem = pl.BlockSpec(memory_space=pltpu.VMEM)
    smem = pl.BlockSpec(memory_space=pltpu.SMEM)
    shape = jax.ShapeDtypeStruct
    hbm = pl.BlockSpec(memory_space=pltpu.HBM)
    qv, kv, gh, s0, p0 = pl.pallas_call(
        own_kernel,
        out_shape=(pltpu.VMEM((heads, width, tok), BF), pltpu.VMEM((width, tok), BF), pltpu.VMEM((rows, lat), BF), pltpu.VMEM((tok, rows), F32), pltpu.VMEM((tok, rows), F32)),
        in_specs=[hbm] * 3,
        out_specs=(vmem,) * 5,
        scratch_shapes=[
            pltpu.VMEM((tok, heads, lat), BF),
            pltpu.VMEM((lat // 128, rows, 128), F32),
            pltpu.SemaphoreType.DMA((5 + heads,)),
        ],
        compiler_params=pltpu.CompilerParams(vmem_limit_bytes=16 << 20), name="own",
    )(qt, out_grad, k0)
    params = pltpu.CompilerParams(vmem_limit_bytes=16 << 20)
    s1, p1 = pl.pallas_call(
        mid_kernel,
        out_shape=(pltpu.VMEM((tok, rows), F32), pltpu.VMEM((tok, rows), F32)),
        in_specs=[vmem] * 3,
        out_specs=(vmem,) * 2,
        compiler_params=params,
        name="mid",
    )(qv, gh, k1)
    w, ds, a2 = pl.pallas_call(
        main_kernel,
        out_shape=(
            pltpu.VMEM((3 * tok, rows), BF),
            pltpu.VMEM((3 * tok, rows), BF),
            pltpu.VMEM((tok, width), BF),
        ),
        in_specs=[smem] + [vmem] * 8,
        out_specs=(vmem,) * 3,
        compiler_params=params,
        name="main",
    )(ctx_index.reshape(1), qv, gh, s0, p0, s1, p1, k2, doc_start.reshape(1, tok))
    r2 = shift(a2, -2)
    a1 = pl.pallas_call(
        back_kernel,
        out_shape=pltpu.VMEM((tok, width), BF),
        in_specs=[vmem] * 4,
        out_specs=vmem,
        compiler_params=params,
        name="back",
    )(w, ds, qv, gh)
    r1 = shift(a1, -1)
    own = pl.pallas_call(
        last_kernel, out_shape=pltpu.VMEM((tok, width), F32), in_specs=[vmem] * 4, out_specs=vmem, compiler_params=pltpu.CompilerParams(vmem_limit_bytes=16 << 20), name="last"
    )(w, ds, qv, gh)
    att, dq = pl.pallas_call(
        out_kernel,
        out_shape=(shape((tok, heads, lat), BF), shape((heads, width, tok), BF)),
        in_specs=[vmem] * 5,
        out_specs=(vmem,) * 2,
        scratch_shapes=[pltpu.VMEM((lat // 128, rows, 128), F32)],
        compiler_params=pltpu.CompilerParams(vmem_limit_bytes=16 << 20), name="outs",
    )(w, ds, k2, k1, kv)
    r2, r1 = (pltpu.with_memory_space_constraint(x, pltpu.VMEM) for x in (r2, r1))
    fours = head_count // 2
    owned = pl.pallas_call(
        add_kernel,
        out_shape=pltpu.VMEM((fours, tok // fours, width), BF),
        in_specs=[vmem] * 3,
        out_specs=vmem,
        compiler_params=pltpu.CompilerParams(vmem_limit_bytes=16 << 20),
        name="add",
    )(own, r2, r1)
    groups = [[2 * y + z for y in range(fours)] for z in range(2)]
    pieces = lax.all_to_all(
        owned, "head", 0, 0, axis_index_groups=groups, tiled=True
    )
    halves = jnp.sum(pieces.astype(F32), axis=0).reshape(2, tok // head_count, width)
    z = lax.axis_index("head") % 2
    mine = jnp.where(z == 0, halves[0], halves[1])
    other = jnp.where(z == 0, halves[1], halves[0]).astype(BF)
    pairs = [[2 * y, 2 * y + 1] for y in range(fours)]
    got = lax.all_gather(other, "head", axis_index_groups=pairs)
    d_key = mine + jnp.where(z == 0, got[1], got[0]).astype(F32)
    return (att, jnp.transpose(dq, (2, 0, 1)), d_key)


def solution(mesh):
    return jax.shard_map(
        step,
        mesh=mesh,
        in_specs=(P("ctx", "head", None), P("ctx", None), P("ctx"), P("ctx", "head", None)),
        out_specs=(P("ctx", "head", None), P("ctx", "head", None), P(("ctx", "head"), None)),
        check_vma=False,
    )
```

time: 62.4 us -> 56.9 us (0.912)
  blocking collectives: 0 us -> 13.2 us
  starting transfers between devices: 26.4 us -> 17.5 us
  Pallas kernels: 16.9 us -> 10.7 us
  other arithmetic: 2.35 us -> 0.66 us
  waiting for transfers between devices: 14.9 us -> 13.8 us
  local copies, waits for them, and re-layouts: 0.65 us -> 0.01 us
    all_gather x0 -> x1, blocking collectives: none -> 13.2 us  [step(): got = lax.all_gather(other, 'head', axis_index_groups=pairs)]
    ppermute x1 -> x0, starting transfers between devices: 9.21 us -> none  [shards(): got = lax.ppermute(other, 'head', [(i, i ^ 1) for i in range(head_count)])]
    pallas_call x4 -> x7, Pallas kernels: 16.9 us -> 10.7 us  [the longest x1 3.17 us: step(): pl.pallas_call(own_kernel, out_shape=(pltpu.VMEM((heads, width, tok), BF)...]
    all_to_all x1, waiting for transfers between devices: 6.15 us -> 3.19 us  [step(): lax.all_to_all(owned, 'head', 0, 0, axis_index_groups=groups, tiled=True)]
    ppermute x4, waiting for transfers between devices: 8.07 us -> 10.6 us  [shift(): return lax.ppermute(value, both, ctx_pairs(step, ctx_count, head_count, 16))]
    convert_element_type x2 -> x1, other arithmetic: 1.7 us -> 0.01 us  [step(): other = jnp.where(z == 0, halves[1], halves[0]).astype(BF)]
    ppermute x1 -> x0, waiting for transfers between devices: 0.73 us -> none  [shards(): got = lax.ppermute(other, 'head', [(i, i ^ 1) for i in range(head_count)])]
    unnamed x4 -> x2, local copies, waits for them, and re-layouts: 0.65 us -> 0.01 us
  transfers between devices with their start and end apart: 6 -> 5, of which waited for: 4 -> 4; matrix products, arithmetic and copies ran while one was open for 0% -> 0% of each run, Pallas kernels for 19% -> 13%
where the time goes in v2:
time: 56.9 us; the launch traced here: 56.6 us
  starting transfers between devices  17.5 us (31%)
  waiting for transfers between devices  13.8 us (24%)
  blocking collectives  13.2 us (23%)
  Pallas kernels  10.7 us (19%)
  between operations  0.73 us (1%)
  other arithmetic  0.66 us (1%)
    all_gather x1, blocking collectives, step(): got = lax.all_gather(other, 'head', axis_index_groups=pairs)  13.2 us
    ppermute x4, starting transfers between devices, shift(): return lax.ppermute(value, both, ctx_pairs(step, ctx_count, head_count, 16))  13 us
    ppermute x4, waiting for transfers between devices, shift(): return lax.ppermute(value, both, ctx_pairs(step, ctx_count, head_count, 16))  10.6 us
    all_to_all x1, starting transfers between devices, step(): lax.all_to_all(owned, 'head', 0, 0, axis_index_groups=groups, tiled=True)  4.47 us
    all_to_all x1, waiting for transfers between devices, step(): lax.all_to_all(owned, 'head', 0, 0, axis_index_groups=groups, tiled=True)  3.19 us
    pallas_call x1, Pallas kernels, step(): pl.pallas_call(own_kernel, out_shape=(pltpu.VMEM((heads, width, tok), BF)...  3.17 us
    pallas_call x1, Pallas kernels, step(): pl.pallas_call(out_kernel, out_shape=(shape((tok, heads, lat), BF), shape...  2.96 us
    pallas_call x1, Pallas kernels, step(): pl.pallas_call(main_kernel, out_shape=(pltpu.VMEM((3 * tok, rows), BF), p...  1.87 us
  transfers between devices with their start and end apart: 5, of which 4 were waited for; matrix products, arithmetic and copies ran while one was open for 0% of the time, Pallas kernels for 13%

profile of v2, /device:TPU:6, one launch (start us, length us, event | category | flops | bytes accessed | tf_op | source)
XLA Modules:
  0.0 56.6 jit_solution(10656650756773057814)
XLA Ops:
  0.6 1.9 %collective-permute-start = (bf16[128,576]{0,1:T(8,128)(2,1)}, bf16[128,576]{0,1:T(8,128)(2,1)S(1)}, u32[]{:S(2)}, u32[]{:S(2)}) collective-permute-start(bf16[128,576]{0,1:T(8,128)(2,1)} %param.5), channel_id=1, source_target_pairs={{0,8},{1,9},{2,10},{3,11},{4,12},{5,13},{6,14},{7,15},{8,16},{9,17... | collective-permute-start | bytes 442376 | tf_op jit(solution)/shard_map/ppermute | solution.py:149
  2.6 3.8 %collective-permute-start.1 = (bf16[128,576]{0,1:T(8,128)(2,1)}, bf16[128,576]{0,1:T(8,128)(2,1)S(1)}, u32[]{:S(2)}, u32[]{:S(2)}) collective-permute-start(bf16[128,576]{0,1:T(8,128)(2,1)} %param.5), channel_id=1, source_target_pairs={{0,16},{1,17},{2,18},{3,19},{4,20},{5,21},{6,22},{7,23},{8,24},{9,... | collective-permute-start | bytes 442376 | tf_op jit(solution)/shard_map/ppermute | solution.py:149
  6.4 3.2 %own.1 = (bf16[8,576,128]{2,1,0:T(8,128)(2,1)S(1)}, bf16[576,128]{1,0:T(8,128)(2,1)S(1)}, bf16[1024,512]{1,0:T(8,128)(2,1)S(1)}, f32[128,1024]{1,0:T(8,128)S(1)}, f32[128,1024]{1,0:T(8,128)S(1)}) custom-call(bf16[8,576,128]{2,1,0:T(8,128)(2,1)} %bitcast.12, bf16[128,8,512]{2,1,0:T(8,128)(2,1)} %g_ref.1, bf16[576,128]{1,0:T(8,128)(2,1)} %bitcast.13), custom_call_target="tpu_custom_call" | custom-call | tf_op jit(solution)/shard_map/own/pallas_call | solution.py:162
  9.6 5.2 %collective-permute-done = bf16[128,576]{0,1:T(8,128)(2,1)S(1)} collective-permute-done((bf16[128,576]{0,1:T(8,128)(2,1)}, bf16[128,576]{0,1:T(8,128)(2,1)S(1)}, u32[]{:S(2)}, u32[]{:S(2)}) %collective-permute-start) | collective-permute-done | bytes 147488 | tf_op jit(solution)/shard_map/ppermute | solution.py:149
  14.8 0.0 copy-start
  14.8 0.7 %mid.1 = (f32[128,1024]{1,0:T(8,128)S(1)}, f32[128,1024]{1,0:T(8,128)S(1)}) custom-call(bf16[8,576,128]{2,1,0:T(8,128)(2,1)S(1)} %get-tuple-element.15.q_ref, bf16[1024,512]{1,0:T(8,128)(2,1)S(1)} %get-tuple-element.16.gh_ref, bf16[576,128]{1,0:T(8,128)(2,1)S(1)} %bitcast.7), custom_call_target="tpu_custom_call" | custom-call | tf_op jit(solution)/shard_map/mid/pallas_call | solution.py:175
  15.4 2.8 %collective-permute-done.1 = bf16[128,576]{0,1:T(8,128)(2,1)S(1)} collective-permute-done((bf16[128,576]{0,1:T(8,128)(2,1)}, bf16[128,576]{0,1:T(8,128)(2,1)S(1)}, u32[]{:S(2)}, u32[]{:S(2)}) %collective-permute-start.1) | collective-permute-done | bytes 147488 | tf_op jit(solution)/shard_map/ppermute | solution.py:149
  18.3 0.0 copy-done
  18.3 1.9 %main.1 = (bf16[384,1024]{1,0:T(8,128)(2,1)S(1)}, bf16[384,1024]{1,0:T(8,128)(2,1)S(1)}, bf16[128,576]{1,0:T(8,128)(2,1)S(1)}) custom-call(s32[1]{0:T(128)} %bitcast.ctx_ref, bf16[8,576,128]{2,1,0:T(8,128)(2,1)S(1)} %get-tuple-element.15.q_ref, bf16[1024,512]{1,0:T(8,128)(2,1)S(1)} %get-tuple-element.16.gh_ref, f32[128,1024]{1,0:T(8,128)S(1)} %get-tuple-element.17.s0_ref, ...), custom_call_target="tpu_custom_call" | custom-call | tf_op jit(solution)/shard_map/main/pallas_call | solution.py:183
  20.2 0.7 %back.1 = bf16[128,576]{1,0:T(8,128)(2,1)S(1)} custom-call(bf16[384,1024]{1,0:T(8,128)(2,1)S(1)} %get-tuple-element.21.w_ref, bf16[384,1024]{1,0:T(8,128)(2,1)S(1)} %get-tuple-element.22.ds_ref, bf16[8,576,128]{2,1,0:T(8,128)(2,1)S(1)} %get-tuple-element.15.q_ref, bf16[1024,512]{1,0:T(8,128)(2,1)S(1)} %get-tuple-element.16.gh_ref), custom_call_target="tpu_custom_call" | custom-call | tf_op jit(solution)/shard_map/back/pallas_call | solution.py:196
  20.8 3.3 %collective-permute-start.3 = (bf16[128,576]{1,0:T(8,128)(2,1)S(1)}, bf16[128,576]{1,0:T(8,128)(2,1)S(1)}, u32[]{:S(2)}, u32[]{:S(2)}) collective-permute-start(bf16[128,576]{1,0:T(8,128)(2,1)S(1)} %back.1), channel_id=1, source_target_pairs={{8,0},{9,1},{10,2},{11,3},{12,4},{13,5},{14,6},{15,7},{16,8},{17,9... | collective-permute-start | bytes 442376 | tf_op jit(solution)/shard_map/ppermute | solution.py:149
  24.2 3.9 %collective-permute-start.2 = (bf16[128,576]{1,0:T(8,128)(2,1)S(1)}, bf16[128,576]{1,0:T(8,128)(2,1)S(1)}, u32[]{:S(2)}, u32[]{:S(2)}) collective-permute-start(bf16[128,576]{1,0:T(8,128)(2,1)S(1)} %get-tuple-element.26), channel_id=1, source_target_pairs={{16,0},{17,1},{18,2},{19,3},{20,4},{21,5},{22,6},{23,7},{24,8},{25... | collective-permute-start | bytes 442376 | tf_op jit(solution)/shard_map/ppermute | solution.py:149
  28.1 0.7 %last.1.own_ref = f32[128,576]{1,0:T(8,128)S(1)} custom-call(bf16[384,1024]{1,0:T(8,128)(2,1)S(1)} %get-tuple-element.21.w_ref, bf16[384,1024]{1,0:T(8,128)(2,1)S(1)} %get-tuple-element.22.ds_ref, bf16[8,576,128]{2,1,0:T(8,128)(2,1)S(1)} %get-tuple-element.15.q_ref, bf16[1024,512]{1,0:T(8,128)(2,1)S(1)} %get-tuple-element.16.gh_ref), custom_call_target="tpu_custom_call" | custom-call | tf_op jit(solution)/shard_map/last/pallas_call | solution.py:205
  28.8 0.0 collective-permute-done.3.r1_ref
  28.8 2.6 %collective-permute-done.2.r2_ref = bf16[128,576]{1,0:T(8,128)(2,1)S(1)} collective-permute-done((bf16[128,576]{1,0:T(8,128)(2,1)S(1)}, bf16[128,576]{1,0:T(8,128)(2,1)S(1)}, u32[]{:S(2)}, u32[]{:S(2)}) %collective-permute-start.2) | collective-permute-done | bytes 147488 | tf_op jit(solution)/shard_map/ppermute | solution.py:149
  31.4 0.7 %add.11 = bf16[4,32,576]{2,1,0:T(8,128)(2,1)} custom-call(f32[128,576]{1,0:T(8,128)S(1)} %last.1.own_ref, bf16[128,576]{1,0:T(8,128)(2,1)S(1)} %collective-permute-done.2.r2_ref, bf16[128,576]{1,0:T(8,128)(2,1)S(1)} %collective-permute-done.3.r1_ref), custom_call_target="tpu_custom_call" | custom-call | tf_op jit(solution)/shard_map/add/pallas_call | solution.py:218
  32.1 4.5 %all-to-all-start = ((bf16[4,32,576]{2,1,0:T(8,128)(2,1)}), bf16[4,32,576]{2,1,0:T(8,128)(2,1)S(1)}, u32[]{:S(2)}, u32[]{:S(2)}) async-start(bf16[4,32,576]{2,1,0:T(8,128)(2,1)} %add.11), calls=%async_computation | async-start | bytes 327680 | tf_op jit(solution)/shard_map/all_to_all | solution.py:227
  36.6 3.0 %outs.1 = (bf16[128,8,512]{2,1,0:T(8,128)(2,1)}, bf16[8,576,128]{2,1,0:T(8,128)(2,1)}) custom-call(bf16[384,1024]{1,0:T(8,128)(2,1)S(1)} %get-tuple-element.21.w_ref, bf16[384,1024]{1,0:T(8,128)(2,1)S(1)} %get-tuple-element.22.ds_ref, bf16[576,128]{1,0:T(8,128)(2,1)S(1)} %bitcast.10, bf16[576,128]{1,0:T(8,128)(2,1)S(1)} %bitcast.8, ...), custom_call_target="tpu_custom_call" | custom-call | tf_op jit(solution)/shard_map/outs/pallas_call | solution.py:208
  39.5 3.2 %all-to-all-done = bf16[4,32,576]{2,1,0:T(8,128)(2,1)S(1)} async-done(((bf16[4,32,576]{2,1,0:T(8,128)(2,1)}), bf16[4,32,576]{2,1,0:T(8,128)(2,1)S(1)}, u32[]{:S(2)}, u32[]{:S(2)}) %all-to-all-start) | async-done | bytes 147488 | tf_op jit(solution)/shard_map/all_to_all | solution.py:227
  42.8 13.2 %all-gather = bf16[32,576]{1,0:T(8,128)(2,1)S(1)} all-gather(bf16[16,576]{1,0:T(8,128)(2,1)S(1)} %select_convert_fusion), channel_id=2, replica_groups={{0,1},{2,3},{4,5},{6,7},{8,9},{10,11},{12,13},{14,15},{16,17},{18,19},{..., dimensions={0}, use_global_device_ids=true | all-gather | bytes 55296 | tf_op jit(solution)/shard_map/all_gather | solution.py:235
  55.9 0.6 %convert_add_fusion = f32[16,576]{1,0:T(8,128)} fusion(f32[32,576]{1,0:T(8,128)S(1)} %convert_reduce_fusion, bf16[32,576]{1,0:T(8,128)(2,1)S(1)} %all-gather, pred[]{:T(512)S(6)} %eq.4), kind=kLoop, calls=%fused_computation.1 | loop fusion | flops 36864 | bytes 147457 | tf_op jit(solution)/shard_map/add | solution.py:236
  (2 shorter events, 0.0 us)
Async XLA Ops:
  0.6 14.1 %collective-permute-start = (bf16[128,576]{0,1:T(8,128)(2,1)}, bf16[128,576]{0,1:T(8,128)(2,1)S(1)}, u32[]{:S(2)}, u32[]{:S(2)}) collective-permute-start(bf16[128,576]{0,1:T(8,128)(2,1)} %param.5), channel_id=1, source_target_pairs={{0,8},{1,9},{2,10},{3,11},{4,12},{5,13},{6,14},{7,15},{8,16},{9,17... | collective-permute-start | bytes 442376 | tf_op jit(solution)/shard_map/ppermute | solution.py:149
  2.6 15.7 %collective-permute-start.1 = (bf16[128,576]{0,1:T(8,128)(2,1)}, bf16[128,576]{0,1:T(8,128)(2,1)S(1)}, u32[]{:S(2)}, u32[]{:S(2)}) collective-permute-start(bf16[128,576]{0,1:T(8,128)(2,1)} %param.5), channel_id=1, source_target_pairs={{0,16},{1,17},{2,18},{3,19},{4,20},{5,21},{6,22},{7,23},{8,24},{9,... | collective-permute-start | bytes 442376 | tf_op jit(solution)/shard_map/ppermute | solution.py:149
  14.8 3.5 %copy-start = (s32[128]{0:T(128)S(1)}, s32[128]{0:T(128)}, u32[]{:S(2)}) copy-start(s32[128]{0:T(128)} %param.6) | copy-start | bytes 1540
  20.8 8.0 %collective-permute-start.3 = (bf16[128,576]{1,0:T(8,128)(2,1)S(1)}, bf16[128,576]{1,0:T(8,128)(2,1)S(1)}, u32[]{:S(2)}, u32[]{:S(2)}) collective-permute-start(bf16[128,576]{1,0:T(8,128)(2,1)S(1)} %back.1), channel_id=1, source_target_pairs={{8,0},{9,1},{10,2},{11,3},{12,4},{13,5},{14,6},{15,7},{16,8},{17,9... | collective-permute-start | bytes 442376 | tf_op jit(solution)/shard_map/ppermute | solution.py:149
  24.2 7.2 %collective-permute-start.2 = (bf16[128,576]{1,0:T(8,128)(2,1)S(1)}, bf16[128,576]{1,0:T(8,128)(2,1)S(1)}, u32[]{:S(2)}, u32[]{:S(2)}) collective-permute-start(bf16[128,576]{1,0:T(8,128)(2,1)S(1)} %get-tuple-element.26), channel_id=1, source_target_pairs={{16,0},{17,1},{18,2},{19,3},{20,4},{21,5},{22,6},{23,7},{24,8},{25... | collective-permute-start | bytes 442376 | tf_op jit(solution)/shard_map/ppermute | solution.py:149
  32.1 10.6 %all-to-all-start = ((bf16[4,32,576]{2,1,0:T(8,128)(2,1)}), bf16[4,32,576]{2,1,0:T(8,128)(2,1)S(1)}, u32[]{:S(2)}, u32[]{:S(2)}) async-start(bf16[4,32,576]{2,1,0:T(8,128)(2,1)} %add.11), calls=%async_computation | async-start | bytes 327680 | tf_op jit(solution)/shard_map/all_to_all | solution.py:227

commit v3 on v2

v3 whole, which is shorter than its diff:
```python
import jax
import jax.numpy as jnp
from jax import lax
from jax.experimental import pallas as pl
from jax.experimental.pallas import tpu as pltpu
from jax.sharding import PartitionSpec as P

SCALE = 192 ** (-0.5)
LANES = 128
BF = jnp.bfloat16
F32 = jnp.float32
NT = (((1,), (1,)), ((), ()))
NN = (((1,), (0,)), ((), ()))


def dot(a, b, dims):
    return lax.dot_general(a, b, dims, preferred_element_type=F32)


def two_heads(q_ref, h):
    return jnp.concatenate([q_ref[h], q_ref[h + 1]], axis=1)


def own_kernel(q_ref, g_ref, k_ref, qv_ref, kv_ref, gh_ref, s_ref, p_ref, gbuf, wide, sems):
    heads, _, tok = qv_ref.shape
    lat = gh_ref.shape[1]
    parts = 4
    size = tok // parts
    g_copies = []
    for n in range(parts):
        piece = slice(n * size, (n + 1) * size)
        g_copies.append(pltpu.make_async_copy(g_ref.at[piece], gbuf.at[piece], sems.at[n]))
    q_copies = [pltpu.make_async_copy(q_ref.at[h], qv_ref.at[h], sems.at[parts + h]) for h in range(heads)]
    k_copy = pltpu.make_async_copy(k_ref, kv_ref, sems.at[parts + heads])
    for copy in [k_copy] + g_copies + q_copies:
        copy.start()
    k_copy.wait()
    keys = kv_ref[...].T
    for n in range(parts):
        g_copies[n].wait()
        piece = slice(n * size, (n + 1) * size)
        rows = slice(n * size * heads, (n + 1) * size * heads)
        for c in range(lat // LANES):
            lanes = slice(c * LANES, (c + 1) * LANES)
            wide[c, rows, :] = gbuf[piece, :, lanes].astype(F32).reshape(size * heads, LANES)
    for h in range(0, heads, 2):
        for i in (h, h + 1):
            for c in range(lat // LANES):
                part = wide[c, pl.ds(i, tok, stride=heads), :]
                gh_ref[i * tok : (i + 1) * tok, c * LANES : (c + 1) * LANES] = part.astype(BF)
            q_copies[i].wait()
        cols = slice(h * tok, (h + 2) * tok)
        s_ref[:, cols] = dot(keys, two_heads(qv_ref, h), NN)
        p_ref[:, cols] = dot(keys[:, :lat], gh_ref[cols, :], NT)


def visible(ctx_ref, doc_ref, back, blocks):
    tok = doc_ref.shape[1]
    base = ctx_ref[0] * tok
    dims = (blocks * tok, 2 * tok)
    kpos = base - back * tok + lax.broadcasted_iota(jnp.int32, dims, 0)
    qpos = base + (lax.broadcasted_iota(jnp.int32, dims, 1) % tok)
    doc = jnp.concatenate([doc_ref[...], doc_ref[...]], axis=1)
    return (kpos >= doc) & (kpos <= qpos)


def mid_kernel(ctx_ref, q_ref, gh_ref, s0_ref, p0_ref, k_ref, doc_ref, e_ref, p_ref, top_ref, sum_ref, del_ref):
    heads, _, tok = q_ref.shape
    lat = gh_ref.shape[1]
    keys = k_ref[...].T
    seen = visible(ctx_ref, doc_ref, 1, 2)
    for h in range(0, heads, 2):
        cols = slice(h * tok, (h + 2) * tok)
        s = jnp.concatenate([dot(keys, two_heads(q_ref, h), NN), s0_ref[:, cols]], axis=0) * SCALE
        s = jnp.where(seen, s, -jnp.inf)
        top = jnp.max(s, axis=0, keepdims=True)
        e = jnp.exp(s - top)
        p1 = dot(keys[:, :lat], gh_ref[cols, :], NT)
        dp = jnp.concatenate([p1, p0_ref[:, cols]], axis=0)
        e_ref[:, cols] = e
        p_ref[:, cols] = p1
        top_ref[:, cols] = top
        sum_ref[:, cols] = jnp.sum(e, axis=0, keepdims=True)
        del_ref[:, cols] = jnp.sum(e * dp, axis=0, keepdims=True)


def main_kernel(
    ctx_ref, q_ref, gh_ref, top_ref, sum_ref, del_ref, k2_ref, doc_ref, w_ref, ds_ref, fac_ref, delta_ref, a2_ref
):
    heads, _, tok = q_ref.shape
    lat = gh_ref.shape[1]
    keys = k2_ref[...].T
    seen = visible(ctx_ref, doc_ref, 2, 1)
    for h in range(0, heads, 2):
        cols = slice(h * tok, (h + 2) * tok)
        s = jnp.where(seen, dot(keys, two_heads(q_ref, h), NN) * SCALE, -jnp.inf)
        before = top_ref[:, cols]
        top = jnp.maximum(before, jnp.max(s, axis=0, keepdims=True))
        e = jnp.exp(s - top)
        old = jnp.exp(before - top)
        inv = 1.0 / (old * sum_ref[:, cols] + jnp.sum(e, axis=0, keepdims=True))
        dp = dot(keys[:, :lat], gh_ref[cols, :], NT)
        delta = (old * del_ref[:, cols] + jnp.sum(e * dp, axis=0, keepdims=True)) * inv
        prob = e * inv
        w_ref[:, cols] = prob.astype(BF)
        ds_ref[:, cols] = (SCALE * prob * (dp - delta)).astype(BF)
        fac_ref[:, cols] = old * inv
        delta_ref[:, cols] = delta
    put_packed(partial_grad(w_ref, ds_ref, q_ref, gh_ref), a2_ref, lat)


def partial_grad(w_ref, ds_ref, q_ref, gh_ref):
    heads = q_ref.shape[0]
    lat = gh_ref.shape[1]
    qs = jnp.concatenate([q_ref[h] for h in range(heads)], axis=1)
    score_part = dot(ds_ref[...], qs, NT)
    value_part = dot(w_ref[...], gh_ref[...], NN)
    return score_part[:, :lat] + value_part, score_part[:, lat:]


def put_packed(parts, out_ref, lat):
    main, rest = parts
    tok, width = rest.shape
    fold = LANES // width
    rows = tok // fold
    rest = jnp.concatenate([rest[n * rows : (n + 1) * rows] for n in range(fold)], axis=1)
    count = lat // LANES
    out_ref[:tok, :] = main.astype(BF)
    for n in range(count):
        piece = rest[n * rows // count : (n + 1) * rows // count]
        out_ref[tok:, n * LANES : (n + 1) * LANES] = piece.astype(BF)


def get_packed(ref, tok, width):
    lat = ref.shape[1]
    rest = ref[tok:, :].astype(F32)
    rest = jnp.concatenate([rest[:, n * LANES : (n + 1) * LANES] for n in range(lat // LANES)], axis=0)
    rest = jnp.concatenate([rest[:, n * width : (n + 1) * width] for n in range(LANES // width)], axis=0)
    return ref[:tok, :].astype(F32), rest


def finish(e_ref, p_ref, fac_ref, delta_ref, block, w_ref, ds_ref):
    tok = w_ref.shape[0]
    prob = e_ref[block * tok : (block + 1) * tok, :] * fac_ref[...]
    w_ref[...] = prob.astype(BF)
    ds_ref[...] = (SCALE * prob * (p_ref[...] - delta_ref[...])).astype(BF)


def back_kernel(e_ref, p_ref, fac_ref, delta_ref, q_ref, gh_ref, w_ref, ds_ref, o_ref):
    finish(e_ref, p_ref, fac_ref, delta_ref, 0, w_ref, ds_ref)
    put_packed(partial_grad(w_ref, ds_ref, q_ref, gh_ref), o_ref, gh_ref.shape[1])


def last_kernel(e_ref, p_ref, fac_ref, delta_ref, q_ref, gh_ref, w_ref, ds_ref, o_ref):
    lat = gh_ref.shape[1]
    finish(e_ref, p_ref, fac_ref, delta_ref, 1, w_ref, ds_ref)
    main, rest = partial_grad(w_ref, ds_ref, q_ref, gh_ref)
    o_ref[:, :lat] = main
    o_ref[:, lat:] = rest


def add_kernel(own_ref, r2_ref, r1_ref, o_ref):
    tok, width = own_ref.shape
    lat = r2_ref.shape[1]
    main2, rest2 = get_packed(r2_ref, tok, width - lat)
    main1, rest1 = get_packed(r1_ref, tok, width - lat)
    dims = o_ref.shape[:2]
    o_ref[:, :, :lat] = (own_ref[:, :lat] + main2 + main1).reshape(*dims, lat).astype(BF)
    o_ref[:, :, lat:] = (own_ref[:, lat:] + rest2 + rest1).reshape(*dims, width - lat).astype(BF)


def att_kernel(w2_ref, w1_ref, w0_ref, k2_ref, k1_ref, k0_ref, att_ref, wide):
    tok, heads, lat = att_ref.shape
    kt = jnp.concatenate([k2_ref[:lat], k1_ref[:lat], k0_ref[:lat]], axis=1)
    for i in range(heads):
        cols = slice(i * tok, (i + 1) * tok)
        weights = jnp.concatenate([w2_ref[:, cols].T, w1_ref[:, cols].T, w0_ref[:, cols].T], axis=1)
        att = dot(weights, kt, NT)
        for c in range(lat // LANES):
            wide[c, pl.ds(i, tok, stride=heads), :] = att[:, c * LANES : (c + 1) * LANES]
    for c in range(lat // LANES):
        att_ref[:, :, c * LANES : (c + 1) * LANES] = wide[c].reshape(tok, heads, LANES).astype(BF)


def dq_kernel(ds2_ref, ds1_ref, ds0_ref, k2_ref, k1_ref, k0_ref, dq_ref):
    heads, _, tok = dq_ref.shape
    kt = jnp.concatenate([k2_ref[...], k1_ref[...], k0_ref[...]], axis=1)
    for h in range(0, heads, 2):
        cols = slice(h * tok, (h + 2) * tok)
        ds = jnp.concatenate([ds2_ref[:, cols], ds1_ref[:, cols], ds0_ref[:, cols]], axis=0)
        dq = dot(kt, ds, NN).astype(BF)
        dq_ref[h] = dq[:, :tok]
        dq_ref[h + 1] = dq[:, tok:]


def ctx_pairs(step, ctx_count, head_count, row):
    pairs = []
    for source in range(ctx_count):
        target = source + step
        if 0 <= target < ctx_count:
            flip = source // row != target // row
            for head in range(head_count):
                pairs.append((source * head_count + head, target * head_count + (head ^ 1 if flip else head)))
    return pairs


def in_vmem(*values):
    return tuple(pltpu.with_memory_space_constraint(x, pltpu.VMEM) for x in values)


def call(kernel, out, ins, scratch=()):
    vmem = pl.BlockSpec(memory_space=pltpu.VMEM)
    specs = {"smem": pl.BlockSpec(memory_space=pltpu.SMEM), "hbm": pl.BlockSpec(memory_space=pltpu.HBM)}
    return pl.pallas_call(
        kernel,
        out_shape=out,
        in_specs=[specs.get(where, vmem) for where, _ in ins],
        out_specs=jax.tree.map(lambda _: vmem, out),
        scratch_shapes=scratch,
        compiler_params=pltpu.CompilerParams(vmem_limit_bytes=16 << 20),
    )(*[value for _, value in ins])


def v(*values):
    return [("vmem", value) for value in values]


def step(query_heads, key_latent, doc_start, out_grad):
    tok, heads, width = query_heads.shape
    lat = out_grad.shape[2]
    ctx_count = lax.axis_size("ctx")
    head_count = lax.axis_size("head")
    both = ("ctx", "head")
    rows = tok * heads
    packed = (tok * width // lat, lat)
    mem = pltpu.VMEM
    shape = jax.ShapeDtypeStruct

    def shift(value, steps):
        return lax.ppermute(value, both, ctx_pairs(steps, ctx_count, head_count, 16))

    ctx = ("smem", lax.axis_index("ctx").astype(jnp.int32).reshape(1))
    doc = doc_start.reshape(1, tok)
    kt = key_latent.T
    k1 = shift(kt, 1)
    k2 = shift(kt, 2)
    k2, k1 = in_vmem(k2, k1)
    qt = jnp.transpose(query_heads, (1, 2, 0))
    qt, og, kt = (pltpu.with_memory_space_constraint(x, pltpu.HBM) for x in (qt, out_grad, kt))
    wide_buf = mem((lat // LANES, rows, LANES), F32)
    qv, k0, gh, s0, p0 = call(
        own_kernel,
        (
            mem((heads, width, tok), BF),
            mem((width, tok), BF),
            mem((rows, lat), BF),
            mem((tok, rows), F32),
            mem((tok, rows), F32),
        ),
        [("hbm", qt), ("hbm", og), ("hbm", kt)],
        (mem((tok, heads, lat), BF), wide_buf, pltpu.SemaphoreType.DMA((5 + heads,))),
    )
    row = mem((1, rows), F32)
    e, p1, top, total, part = call(
        mid_kernel,
        (mem((2 * tok, rows), F32), mem((tok, rows), F32), row, row, row),
        [ctx] + v(qv, gh, s0, p0, k1, doc),
    )
    tile = mem((tok, rows), BF)
    w2, ds2, fac, delta, a2 = call(
        main_kernel, (tile, tile, row, row, mem(packed, BF)), [ctx] + v(qv, gh, top, total, part, k2, doc)
    )
    r2 = shift(a2, -2)
    w1, ds1, a1 = call(back_kernel, (tile, tile, mem(packed, BF)), v(e, p1, fac, delta, qv, gh))
    r1 = shift(a1, -1)
    w0, ds0, own = call(last_kernel, (tile, tile, mem((tok, width), F32)), v(e, p0, fac, delta, qv, gh))
    att = call(att_kernel, shape((tok, heads, lat), BF), v(w2, w1, w0, k2, k1, k0), (wide_buf,))
    dq = call(dq_kernel, shape((heads, width, tok), BF), v(ds2, ds1, ds0, k2, k1, k0))
    r2, r1 = in_vmem(r2, r1)
    fours = head_count // 2
    owned = call(add_kernel, mem((fours, tok // fours, width), BF), v(own, r2, r1))
    groups = [[2 * y + z for y in range(fours)] for z in range(2)]
    pieces = lax.all_to_all(owned, "head", 0, 0, axis_index_groups=groups, tiled=True)
    halves = jnp.sum(pieces.astype(F32), axis=0).reshape(2, tok // head_count, width)
    z = lax.axis_index("head") % 2
    mine = jnp.where(z == 0, halves[0], halves[1])
    other = jnp.where(z == 0, halves[1], halves[0]).astype(BF)
    pairs = [[2 * y, 2 * y + 1] for y in range(fours)]
    got = lax.all_gather(other, "head", axis_index_groups=pairs)
    d_key = mine + jnp.where(z == 0, got[1], got[0]).astype(F32)
    return (att, jnp.transpose(dq, (2, 0, 1)), d_key)


def solution(mesh):
    return jax.shard_map(
        step,
        mesh=mesh,
        in_specs=(P("ctx", "head", None), P("ctx", None), P("ctx"), P("ctx", "head", None)),
        out_specs=(P("ctx", "head", None), P("ctx", "head", None), P(("ctx", "head"), None)),
        check_vma=False,
    )
```

time: 56.9 us -> 56.1 us (0.986)
  waiting for transfers between devices: 13.8 us -> 12.3 us
  Pallas kernels: 10.7 us -> 11.5 us
    all_to_all x1, waiting for transfers between devices: 3.19 us -> 1.97 us  [step(): lax.all_to_all(owned, 'head', 0, 0, axis_index_groups=groups, tiled=True)]
    pallas_call x7 -> x8, Pallas kernels: 10.7 us -> 11.5 us  [call(): pl.pallas_call(kernel, out_shape=out, in_specs=[specs.get(where, vmem) fo...]
  transfers between devices with their start and end apart: 5 -> 5, of which waited for: 4 -> 4; matrix products, arithmetic and copies ran while one was open for 0% -> 0% of each run, Pallas kernels for 13% -> 16%
where the time goes in v3:
time: 56.1 us; the launch traced here: 55.8 us
  starting transfers between devices  17.5 us (31%)
  blocking collectives  13.2 us (24%)
  waiting for transfers between devices  12.3 us (22%)
  Pallas kernels  11.5 us (20%)
  between operations  0.74 us (1%)
  other arithmetic  0.66 us (1%)
    all_gather x1, blocking collectives, step(): got = lax.all_gather(other, 'head', axis_index_groups=pairs)  13.2 us
    ppermute x4, starting transfers between devices, shift(): lax.ppermute(value, both, ctx_pairs(steps, ctx_count, head_count, 16))  13 us
    pallas_call x8, Pallas kernels, call(): pl.pallas_call(kernel, out_shape=out, in_specs=[specs.get(where, vmem) fo...  11.5 us
    ppermute x4, waiting for transfers between devices, shift(): lax.ppermute(value, both, ctx_pairs(steps, ctx_count, head_count, 16))  10.3 us
    all_to_all x1, starting transfers between devices, step(): lax.all_to_all(owned, 'head', 0, 0, axis_index_groups=groups, tiled=True)  4.46 us
    all_to_all x1, waiting for transfers between devices, step(): lax.all_to_all(owned, 'head', 0, 0, axis_index_groups=groups, tiled=True)  1.97 us
  transfers between devices with their start and end apart: 5, of which 4 were waited for; matrix products, arithmetic and copies ran while one was open for 0% of the time, Pallas kernels for 16%

profile of v3, /device:TPU:6, one launch (start us, length us, event | category | flops | bytes accessed | tf_op | source)
XLA Modules:
  0.0 55.8 jit_solution(9880700467106993508)
XLA Ops:
  0.6 1.9 %collective-permute-start = (bf16[576,128]{1,0:T(8,128)(2,1)}, bf16[576,128]{1,0:T(8,128)(2,1)S(1)}, u32[]{:S(2)}, u32[]{:S(2)}) collective-permute-start(bf16[576,128]{1,0:T(8,128)(2,1)} %bitcast.9), channel_id=1, source_target_pairs={{0,8},{1,9},{2,10},{3,11},{4,12},{5,13},{6,14},{7,15},{8,16},{9,17... | collective-permute-start | bytes 442376 | tf_op jit(solution)/shard_map/ppermute | solution.py:240
  2.6 3.8 %collective-permute-start.1 = (bf16[576,128]{1,0:T(8,128)(2,1)}, bf16[576,128]{1,0:T(8,128)(2,1)S(1)}, u32[]{:S(2)}, u32[]{:S(2)}) collective-permute-start(bf16[576,128]{1,0:T(8,128)(2,1)} %bitcast.10), channel_id=1, source_target_pairs={{0,16},{1,17},{2,18},{3,19},{4,20},{5,21},{6,22},{7,23},{8,24},{9,... | collective-permute-start | bytes 442376 | tf_op jit(solution)/shard_map/ppermute | solution.py:240
  6.4 0.0 copy-start
  6.4 3.2 %shard_map.67 = (bf16[8,576,128]{2,1,0:T(8,128)(2,1)S(1)}, bf16[576,128]{1,0:T(8,128)(2,1)S(1)}, bf16[1024,512]{1,0:T(8,128)(2,1)S(1)}, f32[128,1024]{1,0:T(8,128)S(1)}, f32[128,1024]{1,0:T(8,128)S(1)}) custom-call(bf16[8,576,128]{2,1,0:T(8,128)(2,1)} %bitcast.7, bf16[128,8,512]{2,1,0:T(8,128)(2,1)} %g_ref.1, bf16[576,128]{1,0:T(8,128)(2,1)} %bitcast.11), custom_call_target="tpu_custom_call" | custom-call | tf_op jit(solution)/shard_map/pallas_call | solution.py:214
  9.6 5.2 %collective-permute-done.k_ref.k1_ref = bf16[576,128]{1,0:T(8,128)(2,1)S(1)} collective-permute-done((bf16[576,128]{1,0:T(8,128)(2,1)}, bf16[576,128]{1,0:T(8,128)(2,1)S(1)}, u32[]{:S(2)}, u32[]{:S(2)}) %collective-permute-start) | collective-permute-done | bytes 147488 | tf_op jit(solution)/shard_map/ppermute | solution.py:240
  14.8 0.0 copy-done
  14.8 0.8 %shard_map.68 = (f32[256,1024]{1,0:T(8,128)S(1)}, f32[128,1024]{1,0:T(8,128)S(1)}, f32[1,1024]{1,0:T(1,128)S(1)}, f32[1,1024]{1,0:T(1,128)S(1)}, f32[1,1024]{1,0:T(1,128)S(1)}) custom-call(s32[1]{0:T(128)} %bitcast.ctx_ref, bf16[8,576,128]{2,1,0:T(8,128)(2,1)S(1)} %get-tuple-element.24.q_ref, bf16[1024,512]{1,0:T(8,128)(2,1)S(1)} %get-tuple-element.25.gh_ref, ...), custom_call_target="tpu_custom_call" | custom-call | tf_op jit(solution)/shard_map/pallas_call | solution.py:214
  15.6 2.7 %collective-permute-done.1.k2_ref = bf16[576,128]{1,0:T(8,128)(2,1)S(1)} collective-permute-done((bf16[576,128]{1,0:T(8,128)(2,1)}, bf16[576,128]{1,0:T(8,128)(2,1)S(1)}, u32[]{:S(2)}, u32[]{:S(2)}) %collective-permute-start.1) | collective-permute-done | bytes 147488 | tf_op jit(solution)/shard_map/ppermute | solution.py:240
  18.3 1.2 %shard_map.69 = (bf16[128,1024]{1,0:T(8,128)(2,1)S(1)}, bf16[128,1024]{1,0:T(8,128)(2,1)S(1)}, f32[1,1024]{1,0:T(1,128)S(1)}, f32[1,1024]{1,0:T(1,128)S(1)}, bf16[144,512]{1,0:T(8,128)(2,1)S(1)}) custom-call(s32[1]{0:T(128)} %bitcast.ctx_ref, bf16[8,576,128]{2,1,0:T(8,128)(2,1)S(1)} %get-tuple-element.24.q_ref, ...), custom_call_target="tpu_custom_call" | custom-call | tf_op jit(solution)/shard_map/pallas_call | solution.py:214
  19.5 0.7 %shard_map.70 = (bf16[128,1024]{1,0:T(8,128)(2,1)S(1)}, bf16[128,1024]{1,0:T(8,128)(2,1)S(1)}, bf16[144,512]{1,0:T(8,128)(2,1)S(1)}) custom-call(f32[256,1024]{1,0:T(8,128)S(1)} %get-tuple-element.32.e_ref, f32[128,1024]{1,0:T(8,128)S(1)} %get-tuple-element.33.p_ref, f32[1,1024]{1,0:T(1,128)S(1)} %get-tuple-element.34.fac_ref, ...), custom_call_target="tpu_custom_call" | custom-call | tf_op jit(solution)/shard_map/pallas_call | solution.py:214
  20.2 3.4 %collective-permute-start.3 = (bf16[144,512]{1,0:T(8,128)(2,1)S(1)}, bf16[144,512]{1,0:T(8,128)(2,1)S(1)}, u32[]{:S(2)}, u32[]{:S(2)}) collective-permute-start(bf16[144,512]{1,0:T(8,128)(2,1)S(1)} %get-tuple-element.44), channel_id=1, source_target_pairs={{8,0},{9,1},{10,2},{11,3},{12,4},{13,5},{14,6},{15,7},{16,8},{17,9... | collective-permute-start | bytes 442376 | tf_op jit(solution)/shard_map/ppermute | solution.py:240
  23.6 3.9 %collective-permute-start.2 = (bf16[144,512]{1,0:T(8,128)(2,1)S(1)}, bf16[144,512]{1,0:T(8,128)(2,1)S(1)}, u32[]{:S(2)}, u32[]{:S(2)}) collective-permute-start(bf16[144,512]{1,0:T(8,128)(2,1)S(1)} %get-tuple-element.43), channel_id=1, source_target_pairs={{16,0},{17,1},{18,2},{19,3},{20,4},{21,5},{22,6},{23,7},{24,8},{25... | collective-permute-start | bytes 442376 | tf_op jit(solution)/shard_map/ppermute | solution.py:240
  27.5 0.7 %shard_map.71 = (bf16[128,1024]{1,0:T(8,128)(2,1)S(1)}, bf16[128,1024]{1,0:T(8,128)(2,1)S(1)}, f32[128,576]{1,0:T(8,128)S(1)}) custom-call(f32[256,1024]{1,0:T(8,128)S(1)} %get-tuple-element.32.e_ref, f32[128,1024]{1,0:T(8,128)S(1)} %get-tuple-element.27.p0_ref.p_ref, f32[1,1024]{1,0:T(1,128)S(1)} %get-tuple-element.34.fac_ref, ...), custom_call_target="tpu_custom_call" | custom-call | tf_op jit(solution)/shard_map/pallas_call | solution.py:214
  28.2 0.0 collective-permute-done.3.r1_ref
  28.2 2.4 %collective-permute-done.2.r2_ref = bf16[144,512]{1,0:T(8,128)(2,1)S(1)} collective-permute-done((bf16[144,512]{1,0:T(8,128)(2,1)S(1)}, bf16[144,512]{1,0:T(8,128)(2,1)S(1)}, u32[]{:S(2)}, u32[]{:S(2)}) %collective-permute-start.2) | collective-permute-done | bytes 147488 | tf_op jit(solution)/shard_map/ppermute | solution.py:240
  30.6 0.7 %shard_map.74 = bf16[4,32,576]{2,1,0:T(8,128)(2,1)} custom-call(f32[128,576]{1,0:T(8,128)S(1)} %get-tuple-element.42.own_ref, bf16[144,512]{1,0:T(8,128)(2,1)S(1)} %collective-permute-done.2.r2_ref, bf16[144,512]{1,0:T(8,128)(2,1)S(1)} %collective-permute-done.3.r1_ref), custom_call_target="tpu_custom_call" | custom-call | tf_op jit(solution)/shard_map/pallas_call | solution.py:214
  31.4 4.5 %all-to-all-start = ((bf16[4,32,576]{2,1,0:T(8,128)(2,1)}), bf16[4,32,576]{2,1,0:T(8,128)(2,1)S(1)}, u32[]{:S(2)}, u32[]{:S(2)}) async-start(bf16[4,32,576]{2,1,0:T(8,128)(2,1)} %shard_map.74), calls=%async_computation | async-start | bytes 327680 | tf_op jit(solution)/shard_map/all_to_all | solution.py:283
  35.8 2.4 %shard_map.72 = bf16[128,8,512]{2,1,0:T(8,128)(2,1)} custom-call(bf16[128,1024]{1,0:T(8,128)(2,1)S(1)} %get-tuple-element.31.w2_ref, bf16[128,1024]{1,0:T(8,128)(2,1)S(1)} %get-tuple-element.36.w1_ref, bf16[128,1024]{1,0:T(8,128)(2,1)S(1)} %get-tuple-element.37.w0_ref, bf16[576,128]{1,0:T(8,128)(2,1)S(1)} %collective-permute-done.1.k2_ref, ...), custom_call_target="tpu_custom_call" | custom-call | tf_op jit(solution)/shard_map/pallas_call | solution.py:214
  38.2 1.8 %shard_map.73 = bf16[8,576,128]{2,1,0:T(8,128)(2,1)} custom-call(bf16[128,1024]{1,0:T(8,128)(2,1)S(1)} %get-tuple-element.39.ds2_ref, bf16[128,1024]{1,0:T(8,128)(2,1)S(1)} %get-tuple-element.40.ds1_ref, bf16[128,1024]{1,0:T(8,128)(2,1)S(1)} %get-tuple-element.41.ds0_ref, bf16[576,128]{1,0:T(8,128)(2,1)S(1)} %collective-permute-done.1.k2_ref, ...), custom_call_target="tpu_custom_call" | custom-call | tf_op jit(solution)/shard_map/pallas_call | solution.py:214
  40.0 2.0 %all-to-all-done = bf16[4,32,576]{2,1,0:T(8,128)(2,1)S(1)} async-done(((bf16[4,32,576]{2,1,0:T(8,128)(2,1)}), bf16[4,32,576]{2,1,0:T(8,128)(2,1)S(1)}, u32[]{:S(2)}, u32[]{:S(2)}) %all-to-all-start) | async-done | bytes 147488 | tf_op jit(solution)/shard_map/all_to_all | solution.py:283
  42.0 13.2 %all-gather = bf16[32,576]{1,0:T(8,128)(2,1)S(1)} all-gather(bf16[16,576]{1,0:T(8,128)(2,1)S(1)} %select_convert_fusion), channel_id=2, replica_groups={{0,1},{2,3},{4,5},{6,7},{8,9},{10,11},{12,13},{14,15},{16,17},{18,19},{..., dimensions={0}, use_global_device_ids=true | all-gather | bytes 55296 | tf_op jit(solution)/shard_map/all_gather | solution.py:289
  55.2 0.6 %convert_add_fusion = f32[16,576]{1,0:T(8,128)} fusion(f32[32,576]{1,0:T(8,128)S(1)} %convert_reduce_fusion, bf16[32,576]{1,0:T(8,128)(2,1)S(1)} %all-gather, pred[]{:T(512)S(6)} %eq.4), kind=kLoop, calls=%fused_computation.1 | loop fusion | flops 36864 | bytes 147457 | tf_op jit(solution)/shard_map/add | solution.py:290
  (2 shorter events, 0.0 us)
Async XLA Ops:
  0.6 14.1 %collective-permute-start = (bf16[576,128]{1,0:T(8,128)(2,1)}, bf16[576,128]{1,0:T(8,128)(2,1)S(1)}, u32[]{:S(2)}, u32[]{:S(2)}) collective-permute-start(bf16[576,128]{1,0:T(8,128)(2,1)} %bitcast.9), channel_id=1, source_target_pairs={{0,8},{1,9},{2,10},{3,11},{4,12},{5,13},{6,14},{7,15},{8,16},{9,17... | collective-permute-start | bytes 442376 | tf_op jit(solution)/shard_map/ppermute | solution.py:240
  2.6 15.7 %collective-permute-start.1 = (bf16[576,128]{1,0:T(8,128)(2,1)}, bf16[576,128]{1,0:T(8,128)(2,1)S(1)}, u32[]{:S(2)}, u32[]{:S(2)}) collective-permute-start(bf16[576,128]{1,0:T(8,128)(2,1)} %bitcast.10), channel_id=1, source_target_pairs={{0,16},{1,17},{2,18},{3,19},{4,20},{5,21},{6,22},{7,23},{8,24},{9,... | collective-permute-start | bytes 442376 | tf_op jit(solution)/shard_map/ppermute | solution.py:240
  6.4 8.4 %copy-start = (s32[128]{0:T(128)S(1)}, s32[128]{0:T(128)}, u32[]{:S(2)}) copy-start(s32[128]{0:T(128)} %param.6) | copy-start | bytes 1540
  20.2 8.0 %collective-permute-start.3 = (bf16[144,512]{1,0:T(8,128)(2,1)S(1)}, bf16[144,512]{1,0:T(8,128)(2,1)S(1)}, u32[]{:S(2)}, u32[]{:S(2)}) collective-permute-start(bf16[144,512]{1,0:T(8,128)(2,1)S(1)} %get-tuple-element.44), channel_id=1, source_target_pairs={{8,0},{9,1},{10,2},{11,3},{12,4},{13,5},{14,6},{15,7},{16,8},{17,9... | collective-permute-start | bytes 442376 | tf_op jit(solution)/shard_map/ppermute | solution.py:240
  23.6 7.0 %collective-permute-start.2 = (bf16[144,512]{1,0:T(8,128)(2,1)S(1)}, bf16[144,512]{1,0:T(8,128)(2,1)S(1)}, u32[]{:S(2)}, u32[]{:S(2)}) collective-permute-start(bf16[144,512]{1,0:T(8,128)(2,1)S(1)} %get-tuple-element.43), channel_id=1, source_target_pairs={{16,0},{17,1},{18,2},{19,3},{20,4},{21,5},{22,6},{23,7},{24,8},{25... | collective-permute-start | bytes 442376 | tf_op jit(solution)/shard_map/ppermute | solution.py:240
  31.4 10.6 %all-to-all-start = ((bf16[4,32,576]{2,1,0:T(8,128)(2,1)}), bf16[4,32,576]{2,1,0:T(8,128)(2,1)S(1)}, u32[]{:S(2)}, u32[]{:S(2)}) async-start(bf16[4,32,576]{2,1,0:T(8,128)(2,1)} %shard_map.74), calls=%async_computation | async-start | bytes 327680 | tf_op jit(solution)/shard_map/all_to_all | solution.py:283

commit v4 on v3

--- a/solution.py
+++ b/solution.py
@@ -54,25 +54,26 @@
         p_ref[:, cols] = dot(keys[:, :lat], gh_ref[cols, :], NT)
 
 
-def visible(ctx_ref, doc_ref, back, blocks):
+def visible(ctx_ref, doc_ref, blocks):
     tok = doc_ref.shape[1]
     base = ctx_ref[0] * tok
-    dims = (blocks * tok, 2 * tok)
-    kpos = base - back * tok + lax.broadcasted_iota(jnp.int32, dims, 0)
-    qpos = base + (lax.broadcasted_iota(jnp.int32, dims, 1) % tok)
+    row = lax.broadcasted_iota(jnp.int32, (tok, 2 * tok), 0)
+    qpos = base + (lax.broadcasted_iota(jnp.int32, (tok, 2 * tok), 1) % tok)
     doc = jnp.concatenate([doc_ref[...], doc_ref[...]], axis=1)
-    return (kpos >= doc) & (kpos <= qpos)
+    seen = [(base - back * tok + row >= doc) & (base - back * tok + row <= qpos) for back in blocks]
+    return seen
 
 
 def mid_kernel(ctx_ref, q_ref, gh_ref, s0_ref, p0_ref, k_ref, doc_ref, e_ref, p_ref, top_ref, sum_ref, del_ref):
     heads, _, tok = q_ref.shape
     lat = gh_ref.shape[1]
     keys = k_ref[...].T
-    seen = visible(ctx_ref, doc_ref, 1, 2)
-    for h in range(0, heads, 2):
-        cols = slice(h * tok, (h + 2) * tok)
-        s = jnp.concatenate([dot(keys, two_heads(q_ref, h), NN), s0_ref[:, cols]], axis=0) * SCALE
-        s = jnp.where(seen, s, -jnp.inf)
+    seen = visible(ctx_ref, doc_ref, (2, 0))
+    for h in range(0, heads, 2):
+        cols = slice(h * tok, (h + 2) * tok)
+        far = jnp.where(seen[0], dot(keys, two_heads(q_ref, h), NN) * SCALE, -jnp.inf)
+        own = jnp.where(seen[1], s0_ref[:, cols] * SCALE, -jnp.inf)
+        s = jnp.concatenate([far, own], axis=0)
         top = jnp.max(s, axis=0, keepdims=True)
         e = jnp.exp(s - top)
         p1 = dot(keys[:, :lat], gh_ref[cols, :], NT)
@@ -85,12 +86,13 @@
 
 
 def main_kernel(
-    ctx_ref, q_ref, gh_ref, top_ref, sum_ref, del_ref, k2_ref, doc_ref, w_ref, ds_ref, fac_ref, delta_ref, a2_ref
+    ctx_ref, q_ref, gh_ref, e_ref, p2_ref, top_ref, sum_ref, del_ref, k1_ref, doc_ref, *outs
 ):
+    w2_ref, ds2_ref, w_ref, ds_ref, fac_ref, delta_ref, a2_ref, a1_ref = outs
     heads, _, tok = q_ref.shape
     lat = gh_ref.shape[1]
-    keys = k2_ref[...].T
-    seen = visible(ctx_ref, doc_ref, 2, 1)
+    keys = k1_ref[...].T
+    (seen,) = visible(ctx_ref, doc_ref, (1,))
     for h in range(0, heads, 2):
         cols = slice(h * tok, (h + 2) * tok)
         s = jnp.where(seen, dot(keys, two_heads(q_ref, h), NN) * SCALE, -jnp.inf)
@@ -106,7 +108,11 @@
         ds_ref[:, cols] = (SCALE * prob * (dp - delta)).astype(BF)
         fac_ref[:, cols] = old * inv
         delta_ref[:, cols] = delta
-    put_packed(partial_grad(w_ref, ds_ref, q_ref, gh_ref), a2_ref, lat)
+        prob = e_ref[:tok, cols] * (old * inv)
+        w2_ref[:, cols] = prob.astype(BF)
+        ds2_ref[:, cols] = (SCALE * prob * (p2_ref[:, cols] - delta)).astype(BF)
+    put_packed(partial_grad(w2_ref, ds2_ref, q_ref, gh_ref), a2_ref, lat)
+    put_packed(partial_grad(w_ref, ds_ref, q_ref, gh_ref), a1_ref, lat)
 
 
 def partial_grad(w_ref, ds_ref, q_ref, gh_ref):
@@ -139,21 +145,12 @@
     return ref[:tok, :].astype(F32), rest
 
 
-def finish(e_ref, p_ref, fac_ref, delta_ref, block, w_ref, ds_ref):
+def last_kernel(e_ref, p_ref, fac_ref, delta_ref, q_ref, gh_ref, w_ref, ds_ref, o_ref):
+    lat = gh_ref.shape[1]
     tok = w_ref.shape[0]
-    prob = e_ref[block * tok : (block + 1) * tok, :] * fac_ref[...]
+    prob = e_ref[tok:, :] * fac_ref[...]
     w_ref[...] = prob.astype(BF)
     ds_ref[...] = (SCALE * prob * (p_ref[...] - delta_ref[...])).astype(BF)
-
-
-def back_kernel(e_ref, p_ref, fac_ref, delta_ref, q_ref, gh_ref, w_ref, ds_ref, o_ref):
-    finish(e_ref, p_ref, fac_ref, delta_ref, 0, w_ref, ds_ref)
-    put_packed(partial_grad(w_ref, ds_ref, q_ref, gh_ref), o_ref, gh_ref.shape[1])
-
-
-def last_kernel(e_ref, p_ref, fac_ref, delta_ref, q_ref, gh_ref, w_ref, ds_ref, o_ref):
-    lat = gh_ref.shape[1]
-    finish(e_ref, p_ref, fac_ref, delta_ref, 1, w_ref, ds_ref)
     main, rest = partial_grad(w_ref, ds_ref, q_ref, gh_ref)
     o_ref[:, :lat] = main
     o_ref[:, lat:] = rest
@@ -242,8 +239,8 @@
     ctx = ("smem", lax.axis_index("ctx").astype(jnp.int32).reshape(1))
     doc = doc_start.reshape(1, tok)
     kt = key_latent.T
+    k2 = shift(kt, 2)
     k1 = shift(kt, 1)
-    k2 = shift(kt, 2)
     k2, k1 = in_vmem(k2, k1)
     qt = jnp.transpose(query_heads, (1, 2, 0))
     qt, og, kt = (pltpu.with_memory_space_constraint(x, pltpu.HBM) for x in (qt, out_grad, kt))
@@ -261,17 +258,18 @@
         (mem((tok, heads, lat), BF), wide_buf, pltpu.SemaphoreType.DMA((5 + heads,))),
     )
     row = mem((1, rows), F32)
-    e, p1, top, total, part = call(
+    e, p2, top, total, part = call(
         mid_kernel,
         (mem((2 * tok, rows), F32), mem((tok, rows), F32), row, row, row),
-        [ctx] + v(qv, gh, s0, p0, k1, doc),
+        [ctx] + v(qv, gh, s0, p0, k2, doc),
     )
     tile = mem((tok, rows), BF)
-    w2, ds2, fac, delta, a2 = call(
-        main_kernel, (tile, tile, row, row, mem(packed, BF)), [ctx] + v(qv, gh, top, total, part, k2, doc)
+    w2, ds2, w1, ds1, fac, delta, a2, a1 = call(
+        main_kernel,
+        (tile, tile, tile, tile, row, row, mem(packed, BF), mem(packed, BF)),
+        [ctx] + v(qv, gh, e, p2, top, total, part, k1, doc),
     )
     r2 = shift(a2, -2)
-    w1, ds1, a1 = call(back_kernel, (tile, tile, mem(packed, BF)), v(e, p1, fac, delta, qv, gh))
     r1 = shift(a1, -1)
     w0, ds0, own = call(last_kernel, (tile, tile, mem((tok, width), F32)), v(e, p0, fac, delta, qv, gh))
     att = call(att_kernel, shape((tok, heads, lat), BF), v(w2, w1, w0, k2, k1, k0), (wide_buf,))

time: 56.1 us -> 53.7 us (0.957)
  starting transfers between devices: 17.5 us -> 15.7 us
  waiting for transfers between devices: 12.3 us -> 11.7 us
    ppermute x4, starting transfers between devices: 13 us -> 11.3 us  [shift(): lax.ppermute(value, both, ctx_pairs(steps, ctx_count, head_count, 16))]
    ppermute x4, waiting for transfers between devices: 10.3 us -> 9.56 us  [shift(): lax.ppermute(value, both, ctx_pairs(steps, ctx_count, head_count, 16))]
    pallas_call x8 -> x7, Pallas kernels: 11.5 us -> 11.4 us  [call(): pl.pallas_call(kernel, out_shape=out, in_specs=[specs.get(where, vmem) fo...]
  transfers between devices with their start and end apart: 5 -> 5, of which waited for: 4 -> 4; matrix products, arithmetic and copies ran while one was open for 0% -> 0% of each run, Pallas kernels for 16% -> 17%
where the time goes in v4:
time: 53.7 us; the launch traced here: 53.4 us
  starting transfers between devices  15.7 us (29%)
  blocking collectives  13.2 us (25%)
  waiting for transfers between devices  11.7 us (22%)
  Pallas kernels  11.4 us (21%)
  between operations  0.73 us (1%)
  other arithmetic  0.66 us (1%)
    all_gather x1, blocking collectives, step(): got = lax.all_gather(other, 'head', axis_index_groups=pairs)  13.2 us
    pallas_call x7, Pallas kernels, call(): pl.pallas_call(kernel, out_shape=out, in_specs=[specs.get(where, vmem) fo...  11.4 us
    ppermute x4, starting transfers between devices, shift(): lax.ppermute(value, both, ctx_pairs(steps, ctx_count, head_count, 16))  11.3 us
    ppermute x4, waiting for transfers between devices, shift(): lax.ppermute(value, both, ctx_pairs(steps, ctx_count, head_count, 16))  9.56 us
    all_to_all x1, starting transfers between devices, step(): lax.all_to_all(owned, 'head', 0, 0, axis_index_groups=groups, tiled=True)  4.47 us
    all_to_all x1, waiting for transfers between devices, step(): lax.all_to_all(owned, 'head', 0, 0, axis_index_groups=groups, tiled=True)  2.18 us
  transfers between devices with their start and end apart: 5, of which 4 were waited for; matrix products, arithmetic and copies ran while one was open for 0% of the time, Pallas kernels for 17%

profile of v4, /device:TPU:6, one launch (start us, length us, event | category | flops | bytes accessed | tf_op | source)
XLA Modules:
  0.0 53.4 jit_solution(14749560402323282626)
XLA Ops:
  0.6 3.8 %collective-permute-start = (bf16[576,128]{1,0:T(8,128)(2,1)}, bf16[576,128]{1,0:T(8,128)(2,1)S(1)}, u32[]{:S(2)}, u32[]{:S(2)}) collective-permute-start(bf16[576,128]{1,0:T(8,128)(2,1)} %bitcast.9), channel_id=1, source_target_pairs={{0,16},{1,17},{2,18},{3,19},{4,20},{5,21},{6,22},{7,23},{8,24},{9,... | collective-permute-start | bytes 442376 | tf_op jit(solution)/shard_map/ppermute | solution.py:237
  4.5 1.9 %collective-permute-start.1 = (bf16[576,128]{1,0:T(8,128)(2,1)}, bf16[576,128]{1,0:T(8,128)(2,1)S(1)}, u32[]{:S(2)}, u32[]{:S(2)}) collective-permute-start(bf16[576,128]{1,0:T(8,128)(2,1)} %bitcast.10), channel_id=1, source_target_pairs={{0,8},{1,9},{2,10},{3,11},{4,12},{5,13},{6,14},{7,15},{8,16},{9,17... | collective-permute-start | bytes 442376 | tf_op jit(solution)/shard_map/ppermute | solution.py:237
  6.4 0.0 copy-start
  6.4 3.2 %shard_map.67 = (bf16[8,576,128]{2,1,0:T(8,128)(2,1)S(1)}, bf16[576,128]{1,0:T(8,128)(2,1)S(1)}, bf16[1024,512]{1,0:T(8,128)(2,1)S(1)}, f32[128,1024]{1,0:T(8,128)S(1)}, f32[128,1024]{1,0:T(8,128)S(1)}) custom-call(bf16[8,576,128]{2,1,0:T(8,128)(2,1)} %bitcast.7, bf16[128,8,512]{2,1,0:T(8,128)(2,1)} %g_ref.1, bf16[576,128]{1,0:T(8,128)(2,1)} %bitcast.11), custom_call_target="tpu_custom_call" | custom-call | tf_op jit(solution)/shard_map/pallas_call | solution.py:211
  9.6 7.6 %collective-permute-done.k_ref.k2_ref = bf16[576,128]{1,0:T(8,128)(2,1)S(1)} collective-permute-done((bf16[576,128]{1,0:T(8,128)(2,1)}, bf16[576,128]{1,0:T(8,128)(2,1)S(1)}, u32[]{:S(2)}, u32[]{:S(2)}) %collective-permute-start) | collective-permute-done | bytes 147488 | tf_op jit(solution)/shard_map/ppermute | solution.py:237
  17.2 0.0 copy-done
  17.2 0.8 %shard_map.68 = (f32[256,1024]{1,0:T(8,128)S(1)}, f32[128,1024]{1,0:T(8,128)S(1)}, f32[1,1024]{1,0:T(1,128)S(1)}, f32[1,1024]{1,0:T(1,128)S(1)}, f32[1,1024]{1,0:T(1,128)S(1)}) custom-call(s32[1]{0:T(128)} %bitcast.ctx_ref, bf16[8,576,128]{2,1,0:T(8,128)(2,1)S(1)} %get-tuple-element.24.q_ref, bf16[1024,512]{1,0:T(8,128)(2,1)S(1)} %get-tuple-element.25.gh_ref, ...), custom_call_target="tpu_custom_call" | custom-call | tf_op jit(solution)/shard_map/pallas_call | solution.py:211
  18.0 0.0 collective-permute-done.1.k1_ref
  18.0 1.8 %shard_map.69 = (bf16[128,1024]{1,0:T(8,128)(2,1)S(1)}, bf16[128,1024]{1,0:T(8,128)(2,1)S(1)}, bf16[128,1024]{1,0:T(8,128)(2,1)S(1)}, bf16[128,1024]{1,0:T(8,128...) custom-call(s32[1]{0:T(128)} %bitcast.ctx_ref, ...), custom_call_target="tpu_custom_call" | custom-call | tf_op jit(solution)/shard_map/pallas_call | solution.py:211
  19.8 3.6 %collective-permute-start.2 = (bf16[144,512]{1,0:T(8,128)(2,1)S(1)}, bf16[144,512]{1,0:T(8,128)(2,1)S(1)}, u32[]{:S(2)}, u32[]{:S(2)}) collective-permute-start(bf16[144,512]{1,0:T(8,128)(2,1)S(1)} %get-tuple-element.43), channel_id=1, source_target_pairs={{16,0},{17,1},{18,2},{19,3},{20,4},{21,5},{22,6},{23,7},{24,8},{25... | collective-permute-start | bytes 442376 | tf_op jit(solution)/shard_map/ppermute | solution.py:237
  23.4 2.0 %collective-permute-start.3 = (bf16[144,512]{1,0:T(8,128)(2,1)S(1)}, bf16[144,512]{1,0:T(8,128)(2,1)S(1)}, u32[]{:S(2)}, u32[]{:S(2)}) collective-permute-start(bf16[144,512]{1,0:T(8,128)(2,1)S(1)} %get-tuple-element.44), channel_id=1, source_target_pairs={{8,0},{9,1},{10,2},{11,3},{12,4},{13,5},{14,6},{15,7},{16,8},{17,9... | collective-permute-start | bytes 442376 | tf_op jit(solution)/shard_map/ppermute | solution.py:237
  25.4 0.7 %shard_map.70 = (bf16[128,1024]{1,0:T(8,128)(2,1)S(1)}, bf16[128,1024]{1,0:T(8,128)(2,1)S(1)}, f32[128,576]{1,0:T(8,128)S(1)}) custom-call(f32[256,1024]{1,0:T(8,128)S(1)} %get-tuple-element.28.e_ref, f32[128,1024]{1,0:T(8,128)S(1)} %get-tuple-element.27.p0_ref.p_ref, f32[1,1024]{1,0:T(1,128)S(1)} %get-tuple-element.35.fac_ref, ...), custom_call_target="tpu_custom_call" | custom-call | tf_op jit(solution)/shard_map/pallas_call | solution.py:211
  26.1 0.8 %collective-permute-done.2.r2_ref = bf16[144,512]{1,0:T(8,128)(2,1)S(1)} collective-permute-done((bf16[144,512]{1,0:T(8,128)(2,1)S(1)}, bf16[144,512]{1,0:T(8,128)(2,1)S(1)}, u32[]{:S(2)}, u32[]{:S(2)}) %collective-permute-start.2) | collective-permute-done | bytes 147488 | tf_op jit(solution)/shard_map/ppermute | solution.py:237
  26.8 1.2 %collective-permute-done.3.r1_ref = bf16[144,512]{1,0:T(8,128)(2,1)S(1)} collective-permute-done((bf16[144,512]{1,0:T(8,128)(2,1)S(1)}, bf16[144,512]{1,0:T(8,128)(2,1)S(1)}, u32[]{:S(2)}, u32[]{:S(2)}) %collective-permute-start.3) | collective-permute-done | bytes 147488 | tf_op jit(solution)/shard_map/ppermute | solution.py:237
  28.0 0.7 %shard_map.73 = bf16[4,32,576]{2,1,0:T(8,128)(2,1)} custom-call(f32[128,576]{1,0:T(8,128)S(1)} %get-tuple-element.42.own_ref, bf16[144,512]{1,0:T(8,128)(2,1)S(1)} %collective-permute-done.2.r2_ref, bf16[144,512]{1,0:T(8,128)(2,1)S(1)} %collective-permute-done.3.r1_ref), custom_call_target="tpu_custom_call" | custom-call | tf_op jit(solution)/shard_map/pallas_call | solution.py:211
  28.7 4.5 %all-to-all-start = ((bf16[4,32,576]{2,1,0:T(8,128)(2,1)}), bf16[4,32,576]{2,1,0:T(8,128)(2,1)S(1)}, u32[]{:S(2)}, u32[]{:S(2)}) async-start(bf16[4,32,576]{2,1,0:T(8,128)(2,1)} %shard_map.73), calls=%async_computation | async-start | bytes 327680 | tf_op jit(solution)/shard_map/all_to_all | solution.py:281
  33.2 2.4 %shard_map.71 = bf16[128,8,512]{2,1,0:T(8,128)(2,1)} custom-call(bf16[128,1024]{1,0:T(8,128)(2,1)S(1)} %get-tuple-element.33.w2_ref, bf16[128,1024]{1,0:T(8,128)(2,1)S(1)} %get-tuple-element.34.w1_ref, bf16[128,1024]{1,0:T(8,128)(2,1)S(1)} %get-tuple-element.37.w0_ref, bf16[576,128]{1,0:T(8,128)(2,1)S(1)} %collective-permute-done.k_ref.k2_ref, ...), custom_call_target="tpu_custom_call" | custom-call | tf_op jit(solution)/shard_map/pallas_call | solution.py:211
  35.6 1.8 %shard_map.72 = bf16[8,576,128]{2,1,0:T(8,128)(2,1)} custom-call(bf16[128,1024]{1,0:T(8,128)(2,1)S(1)} %get-tuple-element.39.ds2_ref, bf16[128,1024]{1,0:T(8,128)(2,1)S(1)} %get-tuple-element.40.ds1_ref, bf16[128,1024]{1,0:T(8,128)(2,1)S(1)} %get-tuple-element.41.ds0_ref, bf16[576,128]{1,0:T(8,128)(2,1)S(1)} %collective-permute-done.k_ref.k2_ref, ...), custom_call_target="tpu_custom_call" | custom-call | tf_op jit(solution)/shard_map/pallas_call | solution.py:211
  37.4 2.2 %all-to-all-done = bf16[4,32,576]{2,1,0:T(8,128)(2,1)S(1)} async-done(((bf16[4,32,576]{2,1,0:T(8,128)(2,1)}), bf16[4,32,576]{2,1,0:T(8,128)(2,1)S(1)}, u32[]{:S(2)}, u32[]{:S(2)}) %all-to-all-start) | async-done | bytes 147488 | tf_op jit(solution)/shard_map/all_to_all | solution.py:281
  39.6 13.2 %all-gather = bf16[32,576]{1,0:T(8,128)(2,1)S(1)} all-gather(bf16[16,576]{1,0:T(8,128)(2,1)S(1)} %select_convert_fusion), channel_id=2, replica_groups={{0,1},{2,3},{4,5},{6,7},{8,9},{10,11},{12,13},{14,15},{16,17},{18,19},{..., dimensions={0}, use_global_device_ids=true | all-gather | bytes 55296 | tf_op jit(solution)/shard_map/all_gather | solution.py:287
  52.8 0.6 %convert_add_fusion = f32[16,576]{1,0:T(8,128)} fusion(f32[32,576]{1,0:T(8,128)S(1)} %convert_reduce_fusion, bf16[32,576]{1,0:T(8,128)(2,1)S(1)} %all-gather, pred[]{:T(512)S(6)} %eq.4), kind=kLoop, calls=%fused_computation.1 | loop fusion | flops 36864 | bytes 147457 | tf_op jit(solution)/shard_map/add | solution.py:288
  (2 shorter events, 0.0 us)
Async XLA Ops:
  0.6 16.6 %collective-permute-start = (bf16[576,128]{1,0:T(8,128)(2,1)}, bf16[576,128]{1,0:T(8,128)(2,1)S(1)}, u32[]{:S(2)}, u32[]{:S(2)}) collective-permute-start(bf16[576,128]{1,0:T(8,128)(2,1)} %bitcast.9), channel_id=1, source_target_pairs={{0,16},{1,17},{2,18},{3,19},{4,20},{5,21},{6,22},{7,23},{8,24},{9,... | collective-permute-start | bytes 442376 | tf_op jit(solution)/shard_map/ppermute | solution.py:237
  4.5 13.5 %collective-permute-start.1 = (bf16[576,128]{1,0:T(8,128)(2,1)}, bf16[576,128]{1,0:T(8,128)(2,1)S(1)}, u32[]{:S(2)}, u32[]{:S(2)}) collective-permute-start(bf16[576,128]{1,0:T(8,128)(2,1)} %bitcast.10), channel_id=1, source_target_pairs={{0,8},{1,9},{2,10},{3,11},{4,12},{5,13},{6,14},{7,15},{8,16},{9,17... | collective-permute-start | bytes 442376 | tf_op jit(solution)/shard_map/ppermute | solution.py:237
  6.4 10.8 %copy-start = (s32[128]{0:T(128)S(1)}, s32[128]{0:T(128)}, u32[]{:S(2)}) copy-start(s32[128]{0:T(128)} %param.6) | copy-start | bytes 1540
  19.8 7.0 %collective-permute-start.2 = (bf16[144,512]{1,0:T(8,128)(2,1)S(1)}, bf16[144,512]{1,0:T(8,128)(2,1)S(1)}, u32[]{:S(2)}, u32[]{:S(2)}) collective-permute-start(bf16[144,512]{1,0:T(8,128)(2,1)S(1)} %get-tuple-element.43), channel_id=1, source_target_pairs={{16,0},{17,1},{18,2},{19,3},{20,4},{21,5},{22,6},{23,7},{24,8},{25... | collective-permute-start | bytes 442376 | tf_op jit(solution)/shard_map/ppermute | solution.py:237
  23.4 4.6 %collective-permute-start.3 = (bf16[144,512]{1,0:T(8,128)(2,1)S(1)}, bf16[144,512]{1,0:T(8,128)(2,1)S(1)}, u32[]{:S(2)}, u32[]{:S(2)}) collective-permute-start(bf16[144,512]{1,0:T(8,128)(2,1)S(1)} %get-tuple-element.44), channel_id=1, source_target_pairs={{8,0},{9,1},{10,2},{11,3},{12,4},{13,5},{14,6},{15,7},{16,8},{17,9... | collective-permute-start | bytes 442376 | tf_op jit(solution)/shard_map/ppermute | solution.py:237
  28.7 10.8 %all-to-all-start = ((bf16[4,32,576]{2,1,0:T(8,128)(2,1)}), bf16[4,32,576]{2,1,0:T(8,128)(2,1)S(1)}, u32[]{:S(2)}, u32[]{:S(2)}) async-start(bf16[4,32,576]{2,1,0:T(8,128)(2,1)} %shard_map.73), calls=%async_computation | async-start | bytes 327680 | tf_op jit(solution)/shard_map/all_to_all | solution.py:281

commit v5 on v4

--- a/solution.py
+++ b/solution.py
@@ -24,34 +24,31 @@
 def own_kernel(q_ref, g_ref, k_ref, qv_ref, kv_ref, gh_ref, s_ref, p_ref, gbuf, wide, sems):
     heads, _, tok = qv_ref.shape
     lat = gh_ref.shape[1]
-    parts = 4
-    size = tok // parts
+    parts = lat // LANES
     g_copies = []
-    for n in range(parts):
-        piece = slice(n * size, (n + 1) * size)
-        g_copies.append(pltpu.make_async_copy(g_ref.at[piece], gbuf.at[piece], sems.at[n]))
+    for c in range(parts):
+        lanes = slice(c * LANES, (c + 1) * LANES)
+        g_copies.append(pltpu.make_async_copy(g_ref.at[:, :, lanes], gbuf.at[:, :, lanes], sems.at[c]))
     q_copies = [pltpu.make_async_copy(q_ref.at[h], qv_ref.at[h], sems.at[parts + h]) for h in range(heads)]
     k_copy = pltpu.make_async_copy(k_ref, kv_ref, sems.at[parts + heads])
     for copy in [k_copy] + g_copies + q_copies:
         copy.start()
     k_copy.wait()
     keys = kv_ref[...].T
-    for n in range(parts):
-        g_copies[n].wait()
-        piece = slice(n * size, (n + 1) * size)
-        rows = slice(n * size * heads, (n + 1) * size * heads)
-        for c in range(lat // LANES):
-            lanes = slice(c * LANES, (c + 1) * LANES)
-            wide[c, rows, :] = gbuf[piece, :, lanes].astype(F32).reshape(size * heads, LANES)
-    for h in range(0, heads, 2):
+    for c in range(parts):
+        g_copies[c].wait()
+        lanes = slice(c * LANES, (c + 1) * LANES)
+        wide[c] = gbuf[:, :, lanes].astype(F32).reshape(tok * heads, LANES)
+        for i in range(heads):
+            gh_ref[i * tok : (i + 1) * tok, lanes] = wide[c, pl.ds(i, tok, stride=heads), :].astype(BF)
+    for h in range(0, heads, 2):
+        cols = slice(h * tok, (h + 2) * tok)
+        p_ref[:, cols] = dot(keys[:, :lat], gh_ref[cols, :], NT)
+    for h in range(0, heads, 2):
+        cols = slice(h * tok, (h + 2) * tok)
         for i in (h, h + 1):
-            for c in range(lat // LANES):
-                part = wide[c, pl.ds(i, tok, stride=heads), :]
-                gh_ref[i * tok : (i + 1) * tok, c * LANES : (c + 1) * LANES] = part.astype(BF)
             q_copies[i].wait()
-        cols = slice(h * tok, (h + 2) * tok)
         s_ref[:, cols] = dot(keys, two_heads(qv_ref, h), NN)
-        p_ref[:, cols] = dot(keys[:, :lat], gh_ref[cols, :], NT)
 
 
 def visible(ctx_ref, doc_ref, blocks):
@@ -88,7 +85,7 @@
 def main_kernel(
     ctx_ref, q_ref, gh_ref, e_ref, p2_ref, top_ref, sum_ref, del_ref, k1_ref, doc_ref, *outs
 ):
-    w2_ref, ds2_ref, w_ref, ds_ref, fac_ref, delta_ref, a2_ref, a1_ref = outs
+    w_ref, ds_ref, fac_ref, delta_ref, a2_ref, a1_ref = outs
     heads, _, tok = q_ref.shape
     lat = gh_ref.shape[1]
     keys = k1_ref[...].T
@@ -104,15 +101,16 @@
         dp = dot(keys[:, :lat], gh_ref[cols, :], NT)
         delta = (old * del_ref[:, cols] + jnp.sum(e * dp, axis=0, keepdims=True)) * inv
         prob = e * inv
-        w_ref[:, cols] = prob.astype(BF)
-        ds_ref[:, cols] = (SCALE * prob * (dp - delta)).astype(BF)
+        w_ref[tok:, cols] = prob.astype(BF)
+        ds_ref[tok:, cols] = (SCALE * prob * (dp - delta)).astype(BF)
         fac_ref[:, cols] = old * inv
         delta_ref[:, cols] = delta
         prob = e_ref[:tok, cols] * (old * inv)
-        w2_ref[:, cols] = prob.astype(BF)
-        ds2_ref[:, cols] = (SCALE * prob * (p2_ref[:, cols] - delta)).astype(BF)
-    put_packed(partial_grad(w2_ref, ds2_ref, q_ref, gh_ref), a2_ref, lat)
-    put_packed(partial_grad(w_ref, ds_ref, q_ref, gh_ref), a1_ref, lat)
+        w_ref[:tok, cols] = prob.astype(BF)
+        ds_ref[:tok, cols] = (SCALE * prob * (p2_ref[:, cols] - delta)).astype(BF)
+    main, rest = partial_grad(w_ref, ds_ref, q_ref, gh_ref)
+    put_packed((main[:tok], rest[:tok]), a2_ref, lat)
+    put_packed((main[tok:], rest[tok:]), a1_ref, lat)
 
 
 def partial_grad(w_ref, ds_ref, q_ref, gh_ref):
@@ -166,12 +164,12 @@
     o_ref[:, :, lat:] = (own_ref[:, lat:] + rest2 + rest1).reshape(*dims, width - lat).astype(BF)
 
 
-def att_kernel(w2_ref, w1_ref, w0_ref, k2_ref, k1_ref, k0_ref, att_ref, wide):
+def att_kernel(w12_ref, w0_ref, k2_ref, k1_ref, k0_ref, att_ref, wide):
     tok, heads, lat = att_ref.shape
     kt = jnp.concatenate([k2_ref[:lat], k1_ref[:lat], k0_ref[:lat]], axis=1)
     for i in range(heads):
         cols = slice(i * tok, (i + 1) * tok)
-        weights = jnp.concatenate([w2_ref[:, cols].T, w1_ref[:, cols].T, w0_ref[:, cols].T], axis=1)
+        weights = jnp.concatenate([w12_ref[:, cols].T, w0_ref[:, cols].T], axis=1)
         att = dot(weights, kt, NT)
         for c in range(lat // LANES):
             wide[c, pl.ds(i, tok, stride=heads), :] = att[:, c * LANES : (c + 1) * LANES]
@@ -179,12 +177,12 @@
         att_ref[:, :, c * LANES : (c + 1) * LANES] = wide[c].reshape(tok, heads, LANES).astype(BF)
 
 
-def dq_kernel(ds2_ref, ds1_ref, ds0_ref, k2_ref, k1_ref, k0_ref, dq_ref):
+def dq_kernel(ds12_ref, ds0_ref, k2_ref, k1_ref, k0_ref, dq_ref):
     heads, _, tok = dq_ref.shape
     kt = jnp.concatenate([k2_ref[...], k1_ref[...], k0_ref[...]], axis=1)
     for h in range(0, heads, 2):
         cols = slice(h * tok, (h + 2) * tok)
-        ds = jnp.concatenate([ds2_ref[:, cols], ds1_ref[:, cols], ds0_ref[:, cols]], axis=0)
+        ds = jnp.concatenate([ds12_ref[:, cols], ds0_ref[:, cols]], axis=0)
         dq = dot(kt, ds, NN).astype(BF)
         dq_ref[h] = dq[:, :tok]
         dq_ref[h + 1] = dq[:, tok:]
@@ -255,7 +253,7 @@
             mem((tok, rows), F32),
         ),
         [("hbm", qt), ("hbm", og), ("hbm", kt)],
-        (mem((tok, heads, lat), BF), wide_buf, pltpu.SemaphoreType.DMA((5 + heads,))),
+        (mem((tok, heads, lat), BF), wide_buf, pltpu.SemaphoreType.DMA((lat // LANES + heads + 1,))),
     )
     row = mem((1, rows), F32)
     e, p2, top, total, part = call(
@@ -264,16 +262,17 @@
         [ctx] + v(qv, gh, s0, p0, k2, doc),
     )
     tile = mem((tok, rows), BF)
-    w2, ds2, w1, ds1, fac, delta, a2, a1 = call(
+    pair = mem((2 * tok, rows), BF)
+    w12, ds12, fac, delta, a2, a1 = call(
         main_kernel,
-        (tile, tile, tile, tile, row, row, mem(packed, BF), mem(packed, BF)),
+        (pair, pair, row, row, mem(packed, BF), mem(packed, BF)),
         [ctx] + v(qv, gh, e, p2, top, total, part, k1, doc),
     )
     r2 = shift(a2, -2)
     r1 = shift(a1, -1)
     w0, ds0, own = call(last_kernel, (tile, tile, mem((tok, width), F32)), v(e, p0, fac, delta, qv, gh))
-    att = call(att_kernel, shape((tok, heads, lat), BF), v(w2, w1, w0, k2, k1, k0), (wide_buf,))
-    dq = call(dq_kernel, shape((heads, width, tok), BF), v(ds2, ds1, ds0, k2, k1, k0))
+    att = call(att_kernel, shape((tok, heads, lat), BF), v(w12, w0, k2, k1, k0), (wide_buf,))
+    dq = call(dq_kernel, shape((heads, width, tok), BF), v(ds12, ds0, k2, k1, k0))
     r2, r1 = in_vmem(r2, r1)
     fours = head_count // 2
     owned = call(add_kernel, mem((fours, tok // fours, width), BF), v(own, r2, r1))

time: 53.7 us -> 53.6 us (level)
  transfers between devices with their start and end apart: 5 -> 5, of which waited for: 4 -> 4; matrix products, arithmetic and copies ran while one was open for 0% -> 0% of each run, Pallas kernels for 17% -> 16%
where the time goes in v5:
time: 53.6 us; the launch traced here: 53.3 us
  starting transfers between devices  15.7 us (29%)
  blocking collectives  13.2 us (25%)
  waiting for transfers between devices  11.9 us (22%)
  Pallas kernels  11.1 us (21%)
  between operations  0.73 us (1%)
  other arithmetic  0.66 us (1%)
    all_gather x1, blocking collectives, step(): got = lax.all_gather(other, 'head', axis_index_groups=pairs)  13.2 us
    ppermute x4, starting transfers between devices, shift(): lax.ppermute(value, both, ctx_pairs(steps, ctx_count, head_count, 16))  11.2 us
    pallas_call x7, Pallas kernels, call(): pl.pallas_call(kernel, out_shape=out, in_specs=[specs.get(where, vmem) fo...  11.1 us
    ppermute x4, waiting for transfers between devices, shift(): lax.ppermute(value, both, ctx_pairs(steps, ctx_count, head_count, 16))  9.66 us
    all_to_all x1, starting transfers between devices, step(): lax.all_to_all(owned, 'head', 0, 0, axis_index_groups=groups, tiled=True)  4.46 us
    all_to_all x1, waiting for transfers between devices, step(): lax.all_to_all(owned, 'head', 0, 0, axis_index_groups=groups, tiled=True)  2.23 us
  transfers between devices with their start and end apart: 5, of which 4 were waited for; matrix products, arithmetic and copies ran while one was open for 0% of the time, Pallas kernels for 16%

profile of v5, /device:TPU:6, one launch (start us, length us, event | category | flops | bytes accessed | tf_op | source)
XLA Modules:
  0.0 53.3 jit_solution(16289504716812975157)
XLA Ops:
  0.6 3.8 %collective-permute-start = (bf16[576,128]{1,0:T(8,128)(2,1)}, bf16[576,128]{1,0:T(8,128)(2,1)S(1)}, u32[]{:S(2)}, u32[]{:S(2)}) collective-permute-start(bf16[576,128]{1,0:T(8,128)(2,1)} %bitcast.9), channel_id=1, source_target_pairs={{0,16},{1,17},{2,18},{3,19},{4,20},{5,21},{6,22},{7,23},{8,24},{9,... | collective-permute-start | bytes 442376 | tf_op jit(solution)/shard_map/ppermute | solution.py:235
  4.5 1.9 %collective-permute-start.1 = (bf16[576,128]{1,0:T(8,128)(2,1)}, bf16[576,128]{1,0:T(8,128)(2,1)S(1)}, u32[]{:S(2)}, u32[]{:S(2)}) collective-permute-start(bf16[576,128]{1,0:T(8,128)(2,1)} %bitcast.10), channel_id=1, source_target_pairs={{0,8},{1,9},{2,10},{3,11},{4,12},{5,13},{6,14},{7,15},{8,16},{9,17... | collective-permute-start | bytes 442376 | tf_op jit(solution)/shard_map/ppermute | solution.py:235
  6.4 0.0 copy-start
  6.4 3.1 %shard_map.67 = (bf16[8,576,128]{2,1,0:T(8,128)(2,1)S(1)}, bf16[576,128]{1,0:T(8,128)(2,1)S(1)}, bf16[1024,512]{1,0:T(8,128)(2,1)S(1)}, f32[128,1024]{1,0:T(8,128)S(1)}, f32[128,1024]{1,0:T(8,128)S(1)}) custom-call(bf16[8,576,128]{2,1,0:T(8,128)(2,1)} %bitcast.7, bf16[128,8,512]{2,1,0:T(8,128)(2,1)} %g_ref.1, bf16[576,128]{1,0:T(8,128)(2,1)} %bitcast.11), custom_call_target="tpu_custom_call" | custom-call | tf_op jit(solution)/shard_map/pallas_call | solution.py:209
  9.5 7.7 %collective-permute-done.k_ref.k2_ref = bf16[576,128]{1,0:T(8,128)(2,1)S(1)} collective-permute-done((bf16[576,128]{1,0:T(8,128)(2,1)}, bf16[576,128]{1,0:T(8,128)(2,1)S(1)}, u32[]{:S(2)}, u32[]{:S(2)}) %collective-permute-start) | collective-permute-done | bytes 147488 | tf_op jit(solution)/shard_map/ppermute | solution.py:235
  17.2 0.0 copy-done
  17.2 0.8 %shard_map.68 = (f32[256,1024]{1,0:T(8,128)S(1)}, f32[128,1024]{1,0:T(8,128)S(1)}, f32[1,1024]{1,0:T(1,128)S(1)}, f32[1,1024]{1,0:T(1,128)S(1)}, f32[1,1024]{1,0:T(1,128)S(1)}) custom-call(s32[1]{0:T(128)} %bitcast.ctx_ref, bf16[8,576,128]{2,1,0:T(8,128)(2,1)S(1)} %get-tuple-element.22.q_ref, bf16[1024,512]{1,0:T(8,128)(2,1)S(1)} %get-tuple-element.23.gh_ref, ...), custom_call_target="tpu_custom_call" | custom-call | tf_op jit(solution)/shard_map/pallas_call | solution.py:209
  18.0 0.0 collective-permute-done.1.k1_ref
  18.0 1.7 %shard_map.69 = (bf16[256,1024]{1,0:T(8,128)(2,1)S(1)}, bf16[256,1024]{1,0:T(8,128)(2,1)S(1)}, f32[1,1024]{1,0:T(1,128)S(1)}, f32[1,1024]{1,0:T(1,128)S(1)}, bf1...) custom-call(s32[1]{0:T(128)} %bitcast.ctx_ref, bf16[8,576,128]{2,1,0:T(8,128)(2,1)S(1)} %get-tuple-element.22.q_ref, ...), custom_call_target="tpu_custom_call" | custom-call | tf_op jit(solution)/shard_map/pallas_call | solution.py:209
  19.7 3.6 %collective-permute-start.2 = (bf16[144,512]{1,0:T(8,128)(2,1)S(1)}, bf16[144,512]{1,0:T(8,128)(2,1)S(1)}, u32[]{:S(2)}, u32[]{:S(2)}) collective-permute-start(bf16[144,512]{1,0:T(8,128)(2,1)S(1)} %get-tuple-element.39), channel_id=1, source_target_pairs={{16,0},{17,1},{18,2},{19,3},{20,4},{21,5},{22,6},{23,7},{24,8},{25... | collective-permute-start | bytes 442376 | tf_op jit(solution)/shard_map/ppermute | solution.py:235
  23.3 1.9 %collective-permute-start.3 = (bf16[144,512]{1,0:T(8,128)(2,1)S(1)}, bf16[144,512]{1,0:T(8,128)(2,1)S(1)}, u32[]{:S(2)}, u32[]{:S(2)}) collective-permute-start(bf16[144,512]{1,0:T(8,128)(2,1)S(1)} %get-tuple-element.40), channel_id=1, source_target_pairs={{8,0},{9,1},{10,2},{11,3},{12,4},{13,5},{14,6},{15,7},{16,8},{17,9... | collective-permute-start | bytes 442376 | tf_op jit(solution)/shard_map/ppermute | solution.py:235
  25.2 0.7 %shard_map.70 = (bf16[128,1024]{1,0:T(8,128)(2,1)S(1)}, bf16[128,1024]{1,0:T(8,128)(2,1)S(1)}, f32[128,576]{1,0:T(8,128)S(1)}) custom-call(f32[256,1024]{1,0:T(8,128)S(1)} %get-tuple-element.26.e_ref, f32[128,1024]{1,0:T(8,128)S(1)} %get-tuple-element.25.p0_ref.p_ref, f32[1,1024]{1,0:T(1,128)S(1)} %get-tuple-element.32.fac_ref, ...), custom_call_target="tpu_custom_call" | custom-call | tf_op jit(solution)/shard_map/pallas_call | solution.py:209
  25.9 0.8 %collective-permute-done.2.r2_ref = bf16[144,512]{1,0:T(8,128)(2,1)S(1)} collective-permute-done((bf16[144,512]{1,0:T(8,128)(2,1)S(1)}, bf16[144,512]{1,0:T(8,128)(2,1)S(1)}, u32[]{:S(2)}, u32[]{:S(2)}) %collective-permute-start.2) | collective-permute-done | bytes 147488 | tf_op jit(solution)/shard_map/ppermute | solution.py:235
  26.7 1.1 %collective-permute-done.3.r1_ref = bf16[144,512]{1,0:T(8,128)(2,1)S(1)} collective-permute-done((bf16[144,512]{1,0:T(8,128)(2,1)S(1)}, bf16[144,512]{1,0:T(8,128)(2,1)S(1)}, u32[]{:S(2)}, u32[]{:S(2)}) %collective-permute-start.3) | collective-permute-done | bytes 147488 | tf_op jit(solution)/shard_map/ppermute | solution.py:235
  27.8 0.7 %shard_map.73 = bf16[4,32,576]{2,1,0:T(8,128)(2,1)} custom-call(f32[128,576]{1,0:T(8,128)S(1)} %get-tuple-element.38.own_ref, bf16[144,512]{1,0:T(8,128)(2,1)S(1)} %collective-permute-done.2.r2_ref, bf16[144,512]{1,0:T(8,128)(2,1)S(1)} %collective-permute-done.3.r1_ref), custom_call_target="tpu_custom_call" | custom-call | tf_op jit(solution)/shard_map/pallas_call | solution.py:209
  28.6 4.5 %all-to-all-start = ((bf16[4,32,576]{2,1,0:T(8,128)(2,1)}), bf16[4,32,576]{2,1,0:T(8,128)(2,1)S(1)}, u32[]{:S(2)}, u32[]{:S(2)}) async-start(bf16[4,32,576]{2,1,0:T(8,128)(2,1)} %shard_map.73), calls=%async_computation | async-start | bytes 327680 | tf_op jit(solution)/shard_map/all_to_all | solution.py:280
  33.0 2.4 %shard_map.71 = bf16[128,8,512]{2,1,0:T(8,128)(2,1)} custom-call(bf16[256,1024]{1,0:T(8,128)(2,1)S(1)} %get-tuple-element.31.w12_ref, bf16[128,1024]{1,0:T(8,128)(2,1)S(1)} %get-tuple-element.34.w0_ref, bf16[576,128]{1,0:T(8,128)(2,1)S(1)} %collective-permute-done.k_ref.k2_ref, bf16[576,128]{1,0:T(8,128)(2,1)S(1)} %collective-permute-done.1.k1_ref, ...), custom_call_target="tpu_custom_call" | custom-call | tf_op jit(solution)/shard_map/pallas_call | solution.py:209
  35.4 1.8 %shard_map.72 = bf16[8,576,128]{2,1,0:T(8,128)(2,1)} custom-call(bf16[256,1024]{1,0:T(8,128)(2,1)S(1)} %get-tuple-element.36.ds12_ref, bf16[128,1024]{1,0:T(8,128)(2,1)S(1)} %get-tuple-element.37.ds0_ref, bf16[576,128]{1,0:T(8,128)(2,1)S(1)} %collective-permute-done.k_ref.k2_ref, bf16[576,128]{1,0:T(8,128)(2,1)S(1)} %collective-permute-done.1.k1_ref, ...), custom_call_target="tpu_custom_call" | custom-call | tf_op jit(solution)/shard_map/pallas_call | solution.py:209
  37.2 2.2 %all-to-all-done = bf16[4,32,576]{2,1,0:T(8,128)(2,1)S(1)} async-done(((bf16[4,32,576]{2,1,0:T(8,128)(2,1)}), bf16[4,32,576]{2,1,0:T(8,128)(2,1)S(1)}, u32[]{:S(2)}, u32[]{:S(2)}) %all-to-all-start) | async-done | bytes 147488 | tf_op jit(solution)/shard_map/all_to_all | solution.py:280
  39.5 13.2 %all-gather = bf16[32,576]{1,0:T(8,128)(2,1)S(1)} all-gather(bf16[16,576]{1,0:T(8,128)(2,1)S(1)} %select_convert_fusion), channel_id=2, replica_groups={{0,1},{2,3},{4,5},{6,7},{8,9},{10,11},{12,13},{14,15},{16,17},{18,19},{..., dimensions={0}, use_global_device_ids=true | all-gather | bytes 55296 | tf_op jit(solution)/shard_map/all_gather | solution.py:286
  52.7 0.6 %convert_add_fusion = f32[16,576]{1,0:T(8,128)} fusion(f32[32,576]{1,0:T(8,128)S(1)} %convert_reduce_fusion, bf16[32,576]{1,0:T(8,128)(2,1)S(1)} %all-gather, pred[]{:T(512)S(6)} %eq.4), kind=kLoop, calls=%fused_computation.1 | loop fusion | flops 36864 | bytes 147457 | tf_op jit(solution)/shard_map/add | solution.py:287
  (2 shorter events, 0.0 us)
Async XLA Ops:
  0.6 16.6 %collective-permute-start = (bf16[576,128]{1,0:T(8,128)(2,1)}, bf16[576,128]{1,0:T(8,128)(2,1)S(1)}, u32[]{:S(2)}, u32[]{:S(2)}) collective-permute-start(bf16[576,128]{1,0:T(8,128)(2,1)} %bitcast.9), channel_id=1, source_target_pairs={{0,16},{1,17},{2,18},{3,19},{4,20},{5,21},{6,22},{7,23},{8,24},{9,... | collective-permute-start | bytes 442376 | tf_op jit(solution)/shard_map/ppermute | solution.py:235
  4.5 13.5 %collective-permute-start.1 = (bf16[576,128]{1,0:T(8,128)(2,1)}, bf16[576,128]{1,0:T(8,128)(2,1)S(1)}, u32[]{:S(2)}, u32[]{:S(2)}) collective-permute-start(bf16[576,128]{1,0:T(8,128)(2,1)} %bitcast.10), channel_id=1, source_target_pairs={{0,8},{1,9},{2,10},{3,11},{4,12},{5,13},{6,14},{7,15},{8,16},{9,17... | collective-permute-start | bytes 442376 | tf_op jit(solution)/shard_map/ppermute | solution.py:235
  6.4 10.8 %copy-start = (s32[128]{0:T(128)S(1)}, s32[128]{0:T(128)}, u32[]{:S(2)}) copy-start(s32[128]{0:T(128)} %param.6) | copy-start | bytes 1540
  19.7 7.0 %collective-permute-start.2 = (bf16[144,512]{1,0:T(8,128)(2,1)S(1)}, bf16[144,512]{1,0:T(8,128)(2,1)S(1)}, u32[]{:S(2)}, u32[]{:S(2)}) collective-permute-start(bf16[144,512]{1,0:T(8,128)(2,1)S(1)} %get-tuple-element.39), channel_id=1, source_target_pairs={{16,0},{17,1},{18,2},{19,3},{20,4},{21,5},{22,6},{23,7},{24,8},{25... | collective-permute-start | bytes 442376 | tf_op jit(solution)/shard_map/ppermute | solution.py:235
  23.3 4.6 %collective-permute-start.3 = (bf16[144,512]{1,0:T(8,128)(2,1)S(1)}, bf16[144,512]{1,0:T(8,128)(2,1)S(1)}, u32[]{:S(2)}, u32[]{:S(2)}) collective-permute-start(bf16[144,512]{1,0:T(8,128)(2,1)S(1)} %get-tuple-element.40), channel_id=1, source_target_pairs={{8,0},{9,1},{10,2},{11,3},{12,4},{13,5},{14,6},{15,7},{16,8},{17,9... | collective-permute-start | bytes 442376 | tf_op jit(solution)/shard_map/ppermute | solution.py:235
  28.6 10.9 %all-to-all-start = ((bf16[4,32,576]{2,1,0:T(8,128)(2,1)}), bf16[4,32,576]{2,1,0:T(8,128)(2,1)S(1)}, u32[]{:S(2)}, u32[]{:S(2)}) async-start(bf16[4,32,576]{2,1,0:T(8,128)(2,1)} %shard_map.73), calls=%async_computation | async-start | bytes 327680 | tf_op jit(solution)/shard_map/all_to_all | solution.py:280
